TPU v7x, 16 devices: a whole 2x2x2 slice. The times are simulated.
16 devices in a mesh: data: 16 (over z, y, x, core).
Axes of the slice: x: 2, y: 2, z: 2, core: 2. Of those that a mesh axis runs over, the one named last changes fastest.
Arguments:
- grad_attn: bfloat16 [16, 12, 589824], P('data')
- grad_mlp: bfloat16 [16, 6, 2359296], P('data')
- grad_wide: bfloat16 [16, 3, 3072], P('data')
- grad_vec: bfloat16 [16, 29, 768], P('data')
- weight_attn: float32 [12, 589824], P(None, 'data')
- weight_mlp: float32 [6, 2359296], P(None, 'data')
- weight_wide: float32 [3, 3072], P(None, 'data')
- weight_vec: float32 [29, 768], P(None, 'data')
- mom1_attn: float32 [12, 589824], P(None, 'data')
- mom1_mlp: float32 [6, 2359296], P(None, 'data')
- mom1_wide: float32 [3, 3072], P(None, 'data')
- mom1_vec: float32 [29, 768], P(None, 'data')
- mom2_attn: float32 [12, 589824], P(None, 'data')
- mom2_mlp: float32 [6, 2359296], P(None, 'data')
- mom2_wide: float32 [3, 3072], P(None, 'data')
- mom2_vec: float32 [29, 768], P(None, 'data')
Outputs:
- output 1: bfloat16 [12, 589824], replicated
- output 2: bfloat16 [6, 2359296], replicated
- output 3: bfloat16 [3, 3072], replicated
- output 4: bfloat16 [29, 768], replicated
- output 5: float32 [12, 589824], P(None, 'data')
- output 6: float32 [6, 2359296], P(None, 'data')
- output 7: float32 [3, 3072], P(None, 'data')
- output 8: float32 [29, 768], P(None, 'data')
- output 9: float32 [12, 589824], P(None, 'data')
- output 10: float32 [6, 2359296], P(None, 'data')
- output 11: float32 [3, 3072], P(None, 'data')
- output 12: float32 [29, 768], P(None, 'data')
- output 13: float32 [12, 589824], P(None, 'data')
- output 14: float32 [6, 2359296], P(None, 'data')
- output 15: float32 [3, 3072], P(None, 'data')
- output 16: float32 [29, 768], P(None, 'data')
All inputs are finite; a program needn't handle non-finite values.
Results may differ from a plain program's by a relative error of at most 0.001.
Values are sent between devices in bfloat16 or wider.
A program may use at most 1 GiB of HBM per device.

v0:
```python
import jax
import jax.numpy as jnp
from jax import lax
from jax.sharding import PartitionSpec as P

STEP_NUMBER = 10
LEARN_RATE = 0.04
BETA_FIRST = 0.9
BETA_SECOND = 0.999
EPSILON = 1e-6
WEIGHT_DECAY = 0.01
MAX_NORM = 1.0


def adam_direction(mean_grad, weight, first_moment, second_moment, clip_coef):
    clipped = clip_coef * mean_grad
    new_first = BETA_FIRST * first_moment + (1.0 - BETA_FIRST) * clipped
    new_second = BETA_SECOND * second_moment + (1.0 - BETA_SECOND) * (clipped * clipped)
    update = (new_first / (1.0 - BETA_FIRST ** STEP_NUMBER)) / (jnp.sqrt(new_second / (1.0 - BETA_SECOND ** STEP_NUMBER)) + EPSILON) + WEIGHT_DECAY * weight
    return update, new_first, new_second


def solution(mesh):
    group_size = mesh.shape["data"]
    grad_spec = P("data", None, None)
    shard_spec = P(None, "data")
    full_spec = P(None, None)

    def local_step(*all_banks):
        grad_banks = all_banks[0:4]
        weights = all_banks[4:8]
        firsts = all_banks[8:12]
        seconds = all_banks[12:16]
        mean_grads = []
        for grad_bank in grad_banks:
            row_count = grad_bank.shape[1]
            shard_width = grad_bank.shape[2] // group_size
            by_owner = grad_bank.reshape(row_count, group_size, shard_width)
            received = lax.all_to_all(by_owner, "data", 1, 1, tiled=True)
            mean_grads.append(jnp.sum(received, axis=1, dtype=jnp.float32) / group_size)
        local_square = sum(jnp.sum(mean_grad * mean_grad) for mean_grad in mean_grads)
        clip_coef = jnp.minimum(1.0, MAX_NORM / jnp.sqrt(lax.psum(local_square, "data")))
        results = [adam_direction(mean_grads[bank_index], weights[bank_index], firsts[bank_index], seconds[bank_index], clip_coef) for bank_index in range(4)]
        part_sums = jnp.concatenate([jnp.sum(weight * weight, axis=1) for weight in weights] + [jnp.sum(result[0] * result[0], axis=1) for result in results])
        norm_sums = lax.psum(part_sums, "data")
        tensor_count = norm_sums.shape[0] // 2
        trust_ratios = jnp.sqrt(norm_sums[:tensor_count]) / jnp.sqrt(norm_sums[tensor_count:])
        replicas, new_weights = [], []
        first_row = 0
        for bank_index in range(4):
            row_count = weights[bank_index].shape[0]
            trust_ratio = trust_ratios[first_row:first_row + row_count]
            first_row = first_row + row_count
            new_weight = weights[bank_index] - LEARN_RATE * trust_ratio[:, None] * results[bank_index][0]
            new_weights.append(new_weight)
            replicas.append(lax.all_gather(new_weight.astype(jnp.bfloat16), "data", axis=1, tiled=True))
        return tuple(replicas + new_weights + [result[1] for result in results] + [result[2] for result in results])

    return jax.shard_map(local_step, mesh=mesh, in_specs=(grad_spec,) * 4 + (shard_spec,) * 12, out_specs=(full_spec,) * 4 + (shard_spec,) * 12, check_vma=False)
```

profile of v0, /device:TPU:0, one launch (start us, length us, event | category | flops | bytes accessed | tf_op | source)
XLA Modules:
  0.0 1114.4 jit_solution(3199196924553498283)
XLA Ops:
  7.2 0.8 reshape.54
  8.7 5.3 all-to-all-start.2
  14.0 1.0 reshape.55
  15.0 0.8 reshape.60
  15.8 3.6 all-to-all-done.2
  19.4 2.2 all-to-all-start.3
  21.6 16.3 %copy.41 = bf16[2,8,16,36864]{3,2,1,0:T(8,128)(2,1)S(1)} copy(bf16[2,8,16,36864]{3,1,2,0:T(8,128)(2,1)} %bitcast.26) | data formatting | bytes 37748736
  38.0 1.7 slice.24
  39.6 11.9 %copy.36 = bf16[12,16,36864]{2,0,1:T(8,128)(2,1)} copy(bf16[12,16,36864]{2,1,0:T(8,128)(2,1)S(1)} %slice.24) | data formatting | bytes 28311552 | tf_op jit(solution)/shard_map/reshape | solution.py:38
  51.5 211.9 %all_to_all.20 = bf16[12,16,36864]{2,0,1:T(8,128)(2,1)} all-to-all(bf16[12,16,36864]{2,0,1:T(8,128)(2,1)} %copy.36), channel_id=1, replica_groups=mesh['data'=16] {'data'}, dimensions={1} | all-to-all | bytes 28311552 | tf_op jit(solution)/shard_map/all_to_all | solution.py:39
  263.3 8.6 all-to-all-start.1
  273.5 10.3 convert_reduce_fusion.1
  283.8 1.2 multiply_reduce_fusion.4
  285.0 437.2 %all-to-all-done.1 = bf16[6,16,147456]{2,0,1:T(8,128)(2,1)} async-done(((bf16[6,16,147456]{2,0,1:T(8,128)(2,1)}), bf16[6,16,147456]{2,0,1:T(8,128)(2,1)}, u32[]{:S(2)}, u32[]{:S(2)}) %all-to-all-start.1) | async-done | bytes 28311584 | tf_op jit(solution)/shard_map/all_to_all | solution.py:39
  722.3 15.0 %convert_reduce_fusion = f32[6,147456]{1,0:T(8,128)} fusion(bf16[6,16,147456]{2,0,1:T(8,128)(2,1)} %all-to-all-done.1), kind=kLoop, calls=%fused_computation | loop fusion | flops 27426816 | bytes 31850496 | tf_op jit(solution)/shard_map/reduce_sum | solution.py:40
  737.2 3.6 multiply_reduce_fusion.1
  743.5 33.1 %psum.14 = f32[]{:T(128)} all-reduce(f32[]{:T(128)S(6)} %add.75), channel_id=1, replica_groups=mesh['data'=16] {'data'}, use_global_device_ids=true, to_apply=%region_12.0 | all-reduce | flops 1 | bytes 8 | tf_op jit(solution)/shard_map/psum | solution.py:42
  777.2 0.7 multiply_reduce_fusion.9
  778.0 11.0 multiply_reduce_fusion
  789.5 4.3 multiply_reduce_fusion.3
  794.0 32.6 %psum.15 = f32[100]{0:T(128)S(1)} all-reduce(f32[100]{0:T(128)S(1)} %concatenate.3), channel_id=1, replica_groups=mesh['data'=16] {'data'}, use_global_device_ids=true, to_apply=%region_17.0 | all-reduce | flops 100 | bytes 800 | tf_op jit(solution)/shard_map/psum | solution.py:45
  826.8 6.2 fusion.1
  833.1 8.2 fusion
  841.4 0.7 convert_bitcast_fusion
  842.0 14.5 %all-gather.1 = bf16[16,48,29]{1,2,0:T(8,128)(2,1)S(1)} all-gather(bf16[1,48,29]{1,2,0:T(8,128)(2,1)S(1)} %get-tuple-element.22), channel_id=1, replica_groups=mesh['data'=16] {'data'}, dimensions={0}, use_global_device_ids=true | all-gather | bytes 47328 | tf_op jit(solution)/shard_map/all_gather | solution.py:56
  856.5 0.8 reshape.59
  858.1 11.8 %all-gather = bf16[16,192,3]{1,2,0:T(4,128)(2,1)S(1)} all-gather(bf16[1,192,3]{1,2,0:T(4,128)(2,1)S(1)} %get-tuple-element.24), channel_id=1, replica_groups=mesh['data'=16] {'data'}, dimensions={0}, use_global_device_ids=true | all-gather | bytes 19584 | tf_op jit(solution)/shard_map/all_gather | solution.py:56
  869.9 0.7 reshape.57
  870.6 47.4 %all-gather.5.cloned.1.call-done = bf16[12,589824]{1,0:T(8,128)(2,1)} async-done(((bf16[12,36864]{1,0:T(8,128)(2,1)}), bf16[12,589824]{1,0:T(8,128)(2,1)}) %all-gather.5.cloned.1.call-update) | async-done | bytes 14155792 | tf_op jit(solution)/shard_map/all_gather | solution.py:56
  918.0 147.8 %all-gather.7.cloned.1.call-done = bf16[6,2359296]{1,0:T(8,128)(2,1)} async-done(((bf16[6,147456]{1,0:T(8,128)(2,1)}), bf16[6,2359296]{1,0:T(8,128)(2,1)}) %all-gather.7.cloned.1.call-update) | async-done | bytes 28311568 | tf_op jit(solution)/shard_map/all_gather | solution.py:56
  1065.7 16.4 %copy.46 = bf16[12,589824]{1,0:T(8,128)(2,1)} copy(bf16[12,589824]{1,0:T(8,128)(2,1)} %all-gather.5.cloned.1.call-done) | data formatting | bytes 28311552
  1082.2 25.4 %copy.47 = bf16[6,2359296]{1,0:T(8,128)(2,1)} copy(bf16[6,2359296]{1,0:T(8,128)(2,1)} %all-gather.7.cloned.1.call-done) | data formatting | bytes 56623104
  (44 shorter events, 3.9 us)
Async XLA Ops:
  8.7 10.7 all-to-all-start.2
  19.4 32.1 %all-to-all-start.3 = ((bf16[16,2,696]{2,1,0:T(2,128)(2,1)}), bf16[16,2,696]{2,1,0:T(2,128)(2,1)S(1)}, u32[]{:S(2)}, u32[]{:S(2)}) async-start(bf16[16,2,696]{2,1,0:T(2,128)(2,1)} %reshape.60), calls=%async_computation.3 | async-start | bytes 98304 | tf_op jit(solution)/shard_map/all_to_all | solution.py:39
  263.3 458.9 %all-to-all-start.1 = ((bf16[6,16,147456]{2,0,1:T(8,128)(2,1)}), bf16[6,16,147456]{2,0,1:T(8,128)(2,1)}, u32[]{:S(2)}, u32[]{:S(2)}) async-start(bf16[6,16,147456]{2,0,1:T(8,128)(2,1)} %bitcast.25), calls=%async_computation.1 | async-start | bytes 75497472 | tf_op jit(solution)/shard_map/all_to_all | solution.py:39
  272.0 646.0 %all-gather.5.cloned.1.call-start = ((), (), s32[]{:S(2)}) async-start(), calls=%async_computation.4 | async-start | bytes 20054016 | tf_op jit(solution)/shard_map/all_gather | solution.py:56
  737.2 40.0 %copy-start.8 = (f32[3,192]{1,0:T(4,128)S(1)}, f32[3,192]{1,0:T(4,128)}, u32[]{:S(2)}) copy-start(f32[3,192]{1,0:T(4,128)} %param.22) | copy-start | bytes 6916
  737.2 40.0 %copy-start.9 = (f32[3,192]{1,0:T(4,128)S(1)}, f32[3,192]{1,0:T(4,128)}, u32[]{:S(2)}) copy-start(f32[3,192]{1,0:T(4,128)} %param.26) | copy-start | bytes 6916
  737.2 40.0 %copy-start.10 = (f32[3,192]{1,0:T(4,128)S(1)}, f32[3,192]{1,0:T(4,128)}, u32[]{:S(2)}) copy-start(f32[3,192]{1,0:T(4,128)} %param.30) | copy-start | bytes 6916
  778.0 11.1 copy-start
  778.0 11.1 copy-start.1
  778.0 11.4 %copy-start.2 = (f32[12,36864]{1,0:T(8,128)S(1)}, f32[12,36864]{1,0:T(8,128)}, u32[]{:S(2)}) copy-start(f32[12,36864]{1,0:T(8,128)} %param.28) | copy-start | bytes 5308420
  789.4 4.3 copy-start.3
  789.4 4.3 copy-start.6
  789.4 4.3 copy-start.7
  793.9 47.4 %copy-start.4 = (f32[29,48]{1,0:T(8,128)}, f32[29,48]{1,0:T(8,128)S(1)}, u32[]{:S(2)}) copy-start(f32[29,48]{1,0:T(8,128)S(1)} %get-tuple-element.68) | copy-start | bytes 16708
  794.0 47.4 %copy-start.5 = (f32[29,48]{1,0:T(8,128)}, f32[29,48]{1,0:T(8,128)S(1)}, u32[]{:S(2)}) copy-start(f32[29,48]{1,0:T(8,128)S(1)} %get-tuple-element.72) | copy-start | bytes 16708
  833.0 232.7 %all-gather.7.cloned.1.call-start = ((), (), s32[]{:S(2)}) async-start(), calls=%async_computation.5 | async-start | bytes 40108032 | tf_op jit(solution)/shard_map/all_gather | solution.py:56
Sparse Core Ops, SparseCore 0:
  833.1 84.7 all-gather.4
  920.8 144.9 all-gather.6
where the time goes:
time: 1120 us; the launch traced here: 1110 us
  waiting for transfers between devices  636 us (57%)
  blocking collectives  304 us (27%)
  local copies, waits for them, and re-layouts  77.2 us (7%)
  other arithmetic  63.6 us (6%)
  between operations  17.5 us (2%)
  starting transfers between devices  16.2 us (1%)
    all_to_all x3, waiting for transfers between devices, local_step(): received = lax.all_to_all(by_owner, 'data', 1, 1, tiled=True)  441 us
    all_to_all x1, blocking collectives, local_step(): received = lax.all_to_all(by_owner, 'data', 1, 1, tiled=True)  212 us
    all_gather x2, waiting for transfers between devices, local_step(): lax.all_gather(new_weight.astype(jnp.bfloat16), 'data', axis=1, tiled=True)  195 us
    unnamed x29, local copies, waits for them, and re-layouts  61.1 us
    psum x1, blocking collectives, local_step(): lax.psum(local_square, 'data')  33.1 us
    psum x1, blocking collectives, local_step(): norm_sums = lax.psum(part_sums, 'data')  32.6 us
    all_gather x2, blocking collectives, local_step(): lax.all_gather(new_weight.astype(jnp.bfloat16), 'data', axis=1, tiled=True)  26.3 us
    reduce_sum x4, other arithmetic, local_step(): mean_grads.append(jnp.sum(received, axis=1, dtype=jnp.float32) / group_size)  25.4 us
  transfers between devices with their start and end apart: 5, of which 4 were waited for; matrix products, arithmetic and copies ran while one was open for 5% of the time, Pallas kernels for 0%

commit v1 on v0

v1 whole, which is shorter than its diff:
```python
import functools

import jax
import jax.numpy as jnp
from jax import lax
from jax.experimental import pallas as pl
from jax.experimental.pallas import tpu as pltpu
from jax.sharding import PartitionSpec as P

STEP_NUMBER = 10
LEARN_RATE = 0.04
BETA_FIRST = 0.9
BETA_SECOND = 0.999
EPSILON = 1e-6
WEIGHT_DECAY = 0.01
MAX_NORM = 1.0
FIRST_SCALE = 1.0 / (1.0 - BETA_FIRST ** STEP_NUMBER)
SECOND_SCALE = 1.0 / (1.0 - BETA_SECOND ** STEP_NUMBER)

MESH = pl.DeviceIdType.MESH
F32 = jnp.float32
BF16 = jnp.bfloat16
DEVICES = 16
LANES = 128
KT = 48
CHUNK = 3 * KT * LANES
ATTN_COLS = 2 * KT * LANES
MLP_COLS = 4 * KT * LANES
ATTN_W = 3 * ATTN_COLS
MLP_W = 6 * MLP_COLS
STEP = 4 * LANES
STEPS = KT * LANES // STEP
TILE = 8
A_ROWS = 12
M_ROWS = 6
GROUPS = 3
PARTS = 3
HALF = LANES // 2
VMEM_LIMIT = 67043328
SMALL = (32, 128)
WEIGHT = (1, 2, 4)
BLOCKS = [slice(row, row + TILE) for row in range(0, SMALL[0], TILE)]
ORDER = [(g, j) for j in range(3) for g in range(3)]
AXES = ((0, 1, 2), (1, 2, 0), (2, 0, 1))


def position():
    me = lax.axis_index("data")
    bits = [lax.rem(me // 2, 2), lax.rem(me // 4, 2), lax.rem(me // 8, 2)]
    return me, lax.rem(me, 2), bits


def flip(bit, by):
    return bit + by - 2 * bit * by


def chip_at(bits, flips):
    total = 0
    for axis in range(3):
        total = total + flip(bits[axis], flips[axis]) * WEIGHT[axis]
    return total


def flips_of(group, first, second, third):
    flips = [0, 0, 0]
    for axis, by in zip(AXES[group], (first, second, third)):
        flips[axis] = by
    return flips


def columns(group, part, owner):
    if part == 0:
        start = owner * ATTN_W + group * ATTN_COLS
        return pl.ds(pl.multiple_of(start, ATTN_COLS), ATTN_COLS)
    start = owner * MLP_W + group * 2 * MLP_COLS + (part - 1) * MLP_COLS
    return pl.ds(pl.multiple_of(start, MLP_COLS), MLP_COLS)


def signal_all(me):
    barrier = pltpu.get_barrier_semaphore()

    @pl.loop(1, DEVICES)
    def _(t):
        pl.semaphore_signal(barrier, inc=1, device_id=(lax.rem(me + t, DEVICES),), device_id_type=MESH)

    pl.semaphore_wait(barrier, DEVICES - 1)


def spread(me, source, slots, send_sem, recv_sem):
    def copy(t):
        peer = lax.rem(me + t, DEVICES)
        return pltpu.make_async_remote_copy(
            src_ref=source(peer), dst_ref=slots.at[me], send_sem=send_sem.at[t], recv_sem=recv_sem.at[me],
            device_id=(peer,), device_id_type=MESH)

    @pl.loop(1, DEVICES)
    def _(t):
        copy(t).start()


def gather_wait(me, source, slots, send_sem, recv_sem):
    @pl.loop(1, DEVICES)
    def _(t):
        peer = lax.rem(me + t, DEVICES)
        pltpu.make_async_remote_copy(
            src_ref=source(peer), dst_ref=slots.at[peer], send_sem=send_sem.at[t], recv_sem=recv_sem.at[peer],
            device_id=(peer,), device_id_type=MESH).wait()


def put_cols(ref, lo, step, value):
    ref[:, pl.ds(pl.multiple_of(lo * LANES + step * STEP, STEP), STEP)] = value


def pack_rows(part, load, put):
    if part == 0:
        a, b = load(0), load(KT)
        put(0, a[0:8])
        put(KT, b[0:8])
        put(2 * KT, jnp.concatenate([a[8:12], b[8:12]], axis=0))
    else:
        d = load(3 * KT)
        for t in range(3):
            put(t * KT, jnp.concatenate([load(t * KT), d[2 * t:2 * t + 2]], axis=0))


def pack_sum(part, own, partner, out, extra):
    @pl.loop(0, STEPS)
    def _(step):
        def cols(lo):
            return pl.ds(pl.multiple_of(lo * LANES + step * STEP, STEP), STEP)

        def put(lo, value):
            if extra is not None:
                value = value + extra[:, cols(lo)]
            put_cols(out, lo, step, value)

        pack_rows(part, lambda lo: own[:, cols(lo)].astype(F32) + partner[:, cols(lo)].astype(F32), put)


def fold(x):
    return sum(x[:, l:l + LANES] for l in range(0, x.shape[1], LANES))


def reduce_kernel(ga, gm, gsmall, pa, pm, gs_a, gs_m, small_out, clip_out,
                  sbuf, r1, r2, r3, raw_a, raw_m, small_slots, norm_slots, acc,
                  d_send, d_recv, s1, q1, s2, q2, s3, q3, load_sem, out_sem, t_send, t_recv, n_send, n_recv):
    me, core, bits = position()
    partner = me + 1 - 2 * core
    signal_all(me)

    def neighbour(axis):
        return me + (2, 4, 8)[axis] * (1 - 2 * bits[axis])


    def owner_chip(half, i, g):
        return chip_at(bits, flips_of(g, 1 - half, 1 - i // 2, 1 - lax.rem(i, 2)))

    def pair_copy(half, i, g, j):
        chip = owner_chip(half, i, g)
        src = (ga, gm)[j > 0].at[0, :, columns(g, j, 2 * chip + 1 - core)]
        dst = (pa, pm)[j > 0].at[:, columns(g, j, chip)]
        return pltpu.make_async_remote_copy(
            src_ref=src, dst_ref=dst, send_sem=d_send.at[half, i, g, j], recv_sem=d_recv.at[half, i, g, j],
            device_id=(partner,), device_id_type=MESH)

    for half in range(2):
        @pl.loop(0, 4)
        def _(i):
            for g, j in ORDER:
                pair_copy(half, i, g, j).start()
        if half == 0:
            spread(me, lambda peer: gsmall.at[peer], small_slots, t_send, t_recv)

    def loads(half, i, g, j, slot):
        chip = owner_chip(half, i, g)
        buf = (raw_a, raw_m)[j > 0]
        own = pltpu.make_async_copy((ga, gm)[j > 0].at[0, :, columns(g, j, 2 * chip + core)], buf.at[slot, 0], load_sem.at[slot, 0])
        par = pltpu.make_async_copy((pa, pm)[j > 0].at[:, columns(g, j, chip)], buf.at[slot, 1], load_sem.at[slot, 1])
        return own, par

    def start_loads(half, i, g, j, slot):
        own, par = loads(half, i, g, j, slot)
        own.start()
        pair_copy(half, i, g, j).wait_recv()
        par.start()

    def send(axis, src, dst, ss, rs):
        return pltpu.make_async_remote_copy(src_ref=src, dst_ref=dst, send_sem=ss, recv_sem=rs,
                                            device_id=(neighbour(axis),), device_id_type=MESH)

    def send1(i, g, j):
        return send(AXES[g][0], sbuf.at[g, i, j], r1.at[g, i, j], s1.at[g, i, j], q1.at[g, i, j])

    def send2(i, g, j):
        return send(AXES[g][1], r1.at[g, i, j], r2.at[g, i, j], s2.at[g, i, j], q2.at[g, i, j])

    def send3(g, j):
        return send(AXES[g][2], r2.at[g, 0, j], r3.at[g, j], s3.at[g, j], q3.at[g, j])

    def sweep(half, i, use):
        start_loads(half, i, *ORDER[0], 0)
        for n, (g, j) in enumerate(ORDER):
            if n + 1 < len(ORDER):
                start_loads(half, i, *ORDER[n + 1], (n + 1) % 2)
            for copy in loads(half, i, g, j, n % 2):
                copy.wait()
            buf = (raw_a, raw_m)[j > 0]
            use(i, g, j, buf.at[n % 2, 0], buf.at[n % 2, 1])

    def first(i, g, j, own, par):
        pack_sum(j, own, par, sbuf.at[g, i, j], None)
        send1(i, g, j).start()

    @pl.loop(0, 4)
    def _(i):
        sweep(0, i, first)

    def second(i, g, j, own, par):
        send1(i, g, j).wait_recv()
        pack_sum(j, own, par, r1.at[g, i, j], r1.at[g, i, j])

    def second_send(i, g, j, own, par):
        second(i, g, j, own, par)
        send2(i, g, j).start()

    @pl.loop(0, 2)
    def _(i):
        sweep(1, i, second_send)

    @pl.loop(2, 4)
    def _(i):
        sweep(1, i, second)

    def add_into(dst, src):
        @pl.loop(0, CHUNK // STEP // 2)
        def _(step):
            cols = pl.ds(pl.multiple_of(step * STEP * 2, STEP * 2), STEP * 2)
            dst[:, cols] = dst[:, cols] + src[:, cols]

    for i in range(2):
        for g, j in ORDER:
            send2(i, g, j).wait_recv()
            add_into(r2.at[g, i, j], r1.at[g, 2 + i, j])
            if i == 0:
                send3(g, j).start()

    gather_wait(me, lambda peer: gsmall.at[peer], small_slots, t_send, t_recv)
    small_slots[me] = gsmall[me]
    small = jnp.zeros(SMALL, F32)
    for slot in range(DEVICES):
        small = small + small_slots[slot].astype(F32)
    small = small * (1.0 / DEVICES)
    small_out[...] = small
    sq = small * small
    acc[...] = sum(sq[rows] for rows in BLOCKS)

    def out_copies(g, j):
        return [pltpu.make_async_copy(r3.at[(g, j) + src], (gs_a, gs_m)[j > 0].at[dst], out_sem.at[g, j, n])
                for n, (src, dst) in enumerate(unpack_moves(g, j, 0))]

    for g, j in ORDER:
        send3(g, j).wait_recv()

        def body(step, sums):
            cols = pl.ds(pl.multiple_of(step * STEP * 2, STEP * 2), STEP * 2)
            value = (r3[g, j, :, cols] + r2[g, 1, j, :, cols]) * (1.0 / DEVICES)
            r3[g, j, :, cols] = value
            return sums + value * value

        sums = lax.fori_loop(0, CHUNK // STEP // 2, body, jnp.zeros((TILE, STEP * 2), F32))
        acc[...] += fold(sums)
        for copy in out_copies(g, j):
            copy.start()

    norm_slots[me] = acc[...]
    spread(me, lambda peer: acc, norm_slots, n_send, n_recv)
    gather_wait(me, lambda peer: acc, norm_slots, n_send, n_recv)
    total = jnp.sum(sum(norm_slots[slot] for slot in range(DEVICES)), axis=(0, 1), keepdims=True)
    clip_out[...] = jnp.broadcast_to(jnp.minimum(1.0, MAX_NORM / jnp.sqrt(total)), (TILE, LANES))

    for g, j in ORDER:
        for copy in out_copies(g, j):
            copy.wait()
        send3(g, j).wait_send()
        for i in range(2):
            send2(i, g, j).wait_send()

    @pl.loop(0, 4)
    def _(i):
        for g, j in ORDER:
            send1(i, g, j).wait_send()
            pair_copy(0, i, g, j).wait_send()
            pair_copy(1, i, g, j).wait_send()


def reduce_call(ga, gm, gsmall):
    hbm = pl.BlockSpec(memory_space=pl.ANY)
    vmem = pl.BlockSpec(memory_space=pltpu.VMEM)
    dma = pltpu.SemaphoreType.DMA
    outs = pl.pallas_call(
        reduce_kernel,
        out_shape=[
            jax.ShapeDtypeStruct((A_ROWS, 8 * ATTN_W), BF16),
            jax.ShapeDtypeStruct((M_ROWS, 8 * MLP_W), BF16),
            jax.ShapeDtypeStruct((A_ROWS, ATTN_W), F32),
            jax.ShapeDtypeStruct((M_ROWS, MLP_W), F32),
            jax.ShapeDtypeStruct(SMALL, F32),
            jax.ShapeDtypeStruct((TILE, LANES), F32),
        ],
        in_specs=[hbm, hbm, vmem],
        out_specs=[hbm] * 4 + [vmem] * 2,
        scratch_shapes=[
            pltpu.VMEM((GROUPS, 4, PARTS, TILE, CHUNK), F32),
            pltpu.VMEM((GROUPS, 4, PARTS, TILE, CHUNK), F32),
            pltpu.VMEM((GROUPS, 2, PARTS, TILE, CHUNK), F32),
            pltpu.VMEM((GROUPS, PARTS, TILE, CHUNK), F32),
            pltpu.VMEM((2, 2, A_ROWS, ATTN_COLS), BF16),
            pltpu.VMEM((2, 2, M_ROWS, MLP_COLS), BF16),
            pltpu.VMEM((DEVICES,) + SMALL, BF16),
            pltpu.VMEM((DEVICES, TILE, LANES), F32),
            pltpu.VMEM((TILE, LANES), F32),
            dma((2, 4, GROUPS, PARTS)), dma((2, 4, GROUPS, PARTS)),
            dma((GROUPS, 4, PARTS)), dma((GROUPS, 4, PARTS)),
            dma((GROUPS, 2, PARTS)), dma((GROUPS, 2, PARTS)),
            dma((GROUPS, PARTS)), dma((GROUPS, PARTS)),
            dma((2, 2)), dma((GROUPS, PARTS, 5)),
            dma((DEVICES,)), dma((DEVICES,)), dma((DEVICES,)), dma((DEVICES,)),
        ],
        compiler_params=pltpu.CompilerParams(collective_id=0, has_side_effects=True, vmem_limit_bytes=VMEM_LIMIT),
        name="reduce_scatter",
    )(ga, gm, gsmall)
    return outs[2:]


def moments(g, m, v, clip):
    return (BETA_FIRST * m + ((1.0 - BETA_FIRST) * clip) * g,
            BETA_SECOND * v + ((1.0 - BETA_SECOND) * (clip * clip)) * (g * g))


def direction(w, new_m, new_v):
    return (new_m * FIRST_SCALE) / (jnp.sqrt(new_v * SECOND_SCALE) + EPSILON) + WEIGHT_DECAY * w


def chunk_columns(g, j):
    n, width = (g, ATTN_COLS) if j == 0 else (2 * g + j - 1, MLP_COLS)
    return n, pl.ds(n * width, width)


def wide_pieces(ref):
    return [ref[rows.start:rows.start + GROUPS, HALF:] for rows in BLOCKS[:GROUPS]]


def update_kernel(*refs):
    banks, (clip, gs_s), vec, wide = (refs[:4], refs[4:8]), refs[8:10], refs[10:13], refs[13:16]
    outs = refs[16:18], refs[18:20]
    small_outs, u_s, w_s, sums = (refs[20:22], refs[22:24]), refs[24], refs[25], (refs[26:28], refs[28:30])
    bufs, load_sem, out_sem = refs[30:32], refs[32], refs[33]

    def loads(g, j):
        n, cols = chunk_columns(g, j)
        return [pltpu.make_async_copy(ref.at[:, cols], bufs[j > 0].at[n, k], load_sem.at[g, j, k]) for k, ref in enumerate(banks[j > 0])]

    def stores(g, j):
        n, cols = chunk_columns(g, j)
        return [pltpu.make_async_copy(bufs[j > 0].at[n, 2 + k], ref.at[:, cols], out_sem.at[g, j, k]) for k, ref in enumerate(outs[j > 0])]

    for g, j in ORDER:
        for copy in loads(g, j):
            copy.start()

    c = clip[0:1, 0:1]
    u_s[...] = jnp.zeros(SMALL, F32)
    w_s[...] = jnp.zeros(SMALL, F32)
    grads = gs_s[0:vec[0].shape[0], 0:vec[0].shape[1]], jnp.concatenate(wide_pieces(gs_s), axis=1)
    for k, (grad, (w, m, v)) in enumerate(zip(grads, (vec, wide))):
        w = w[...]
        new = moments(grad, m[...], v[...], c)
        for ref, value in zip(small_outs[k], new):
            ref[...] = value
        for ref, value in ((u_s, direction(w, *new)), (w_s, w)):
            if k == 0:
                ref[0:value.shape[0], 0:value.shape[1]] = value
            else:
                for t, rows in enumerate(BLOCKS[:GROUPS]):
                    ref[rows.start:rows.start + GROUPS, HALF:] = value[:, t * HALF:(t + 1) * HALF]

    totals = [[jnp.zeros((rows, LANES), F32)] * 2 for rows in (A_ROWS, M_ROWS)]
    for g, j in ORDER:
        for copy in loads(g, j):
            copy.wait()
        buf, n = bufs[j > 0], chunk_columns(g, j)[0]
        width = STEP * (1 + (j > 0))

        def body(step, total):
            cols = pl.ds(pl.multiple_of(step * width, width), width)
            grad, w, m, v = (buf[n, k, :, cols] for k in range(4))
            new = moments(grad, m, v, c)
            for k in range(2):
                buf[n, 2 + k, :, cols] = new[k]
            return tuple(x + fold(y * y) for x, y in zip(total, (direction(w, *new), w)))

        totals[j > 0] = lax.fori_loop(0, buf.shape[3] // width, body, tuple(totals[j > 0]))
        for copy in stores(g, j):
            copy.start()
    for pair, total in zip(sums, totals):
        for ref, value in zip(pair, total):
            ref[...] = value
    for g, j in ORDER:
        for copy in stores(g, j):
            copy.wait()


def update_call(attn, mlp, *small):
    def whole(shape):
        return pl.BlockSpec(shape, lambda n: (0, 0))

    hbm = pl.BlockSpec(memory_space=pl.ANY)
    outs = [small[2].shape] * 2 + [small[5].shape] * 2 + [SMALL] * 2 + [(A_ROWS, LANES)] * 2 + [(M_ROWS, LANES)] * 2
    return pl.pallas_call(
        update_kernel,
        grid=(1,),
        in_specs=[hbm] * 8 + [whole(x.shape) for x in small],
        out_specs=[hbm] * 4 + [whole(shape) for shape in outs],
        out_shape=[jax.ShapeDtypeStruct(shape, F32) for shape in [(A_ROWS, ATTN_W)] * 2 + [(M_ROWS, MLP_W)] * 2 + outs],
        scratch_shapes=[
            pltpu.VMEM((GROUPS, 4, A_ROWS, ATTN_COLS), F32),
            pltpu.VMEM((2 * GROUPS, 4, M_ROWS, MLP_COLS), F32),
            pltpu.SemaphoreType.DMA((GROUPS, PARTS, 4)),
            pltpu.SemaphoreType.DMA((GROUPS, PARTS, 2)),
        ],
        compiler_params=pltpu.CompilerParams(vmem_limit_bytes=VMEM_LIMIT),
        name="update",
    )(*attn, *mlp, *small)


def gather_kernel(*rest):
    banks, rest = (rest[:3], rest[3:6]), rest[6:]
    stats, (full, small_full, nw_a, nw_m, nw_s) = rest[:6], rest[6:11]
    stat_bufs, rest = rest[11:17], rest[17:]
    (sbuf, st_a, st_m, tile, slots, small_buf, x_send, x_recv, d_send, d_recv,
     own_sem, new_sem, load_sem, stat_sem, n_send, n_recv, t_send, t_recv) = rest
    u_s, w_s, uu_a, ww_a, uu_m, ww_m = stat_bufs
    me, core, bits = position()
    partner = me + 1 - 2 * core
    stat_copies = [pltpu.make_async_copy(src, dst, stat_sem.at[n]) for n, (src, dst) in enumerate(zip(stats, stat_bufs))]
    for copy in stat_copies:
        copy.start()
    signal_all(me)

    def chunk(g, j):
        return (st_a, st_m)[j > 0], *chunk_columns(g, j)

    def loads(g, j):
        buf, n, cols = chunk(g, j)
        return [pltpu.make_async_copy(ref.at[:, cols], buf.at[n, k], load_sem.at[g, j, k]) for k, ref in enumerate(banks[j > 0])]

    for copy in stat_copies:
        copy.wait()
    for g, j in ORDER:
        for copy in loads(g, j):
            copy.start()

    lane = lax.broadcasted_iota(jnp.int32, (TILE, LANES), 1)
    out = jnp.zeros((TILE, LANES), F32)

    def pad8(x):
        return jnp.concatenate([x, jnp.zeros((8 - x.shape[0], x.shape[1]), F32)], axis=0)

    for k, (a, m, s) in enumerate([(uu_a, uu_m, u_s), (ww_a, ww_m, w_s)]):
        a, m, s = a[...], m[...], s[...] * s[...]
        vec = jnp.where(lax.broadcasted_iota(jnp.int32, SMALL, 1) < HALF, s, 0.0)
        wide = s - vec
        blocks = [a[0:TILE], pad8(a[TILE:]), pad8(m)] + [vec[rows] for rows in BLOCKS] + [sum(wide[rows] for rows in BLOCKS)]
        for l, block in enumerate(blocks):
            out = jnp.where(lane == TILE * k + l, jnp.sum(block, axis=1, keepdims=True), out)
    tile[...] = out
    slots[me] = out
    spread(me, lambda peer: tile, slots, n_send, n_recv)
    gather_wait(me, lambda peer: tile, slots, n_send, n_recv)
    root = jnp.sqrt(sum(slots[slot] for slot in range(DEVICES)))
    ratio = [LEARN_RATE * (root[:, 8 + l:9 + l] / root[:, l:l + 1]) for l in range(8)]

    def place(g, r, j):
        owner = 2 * chip_at(bits, flips_of(g, lax.rem(r, 2), lax.rem(r // 2, 2), r // 4)) + core
        return full.at[owner, g, j]

    def copy_to(g, r, j, to, arrived, sends, recvs, src):
        return pltpu.make_async_remote_copy(
            src_ref=src, dst_ref=place(g, r, j), send_sem=sends.at[g, arrived, j], recv_sem=recvs.at[g, arrived, j],
            device_id=(to,), device_id_type=MESH)

    def forward(g, r, j, step, src=None):
        axis = AXES[g][step]
        to = me + WEIGHT[axis] * 2 * (1 - 2 * bits[axis])
        copy_to(g, r, j, to, r + WEIGHT[step], x_send, x_recv, place(g, r, j) if src is None else src).start()

    def to_partner(g, r, j, src=None):
        return copy_to(g, r, j, partner, r, d_send, d_recv, place(g, r, j) if src is None else src)

    def arrival(g, r, j):
        return copy_to(g, r, j, partner, r, x_send, x_recv, place(g, r, j))

    def own_copy(g, j):
        return pltpu.make_async_copy(sbuf.at[g, j], place(g, 0, j), own_sem.at[g, j])

    def new_copy(g, j):
        buf, n, cols = chunk(g, j)
        return pltpu.make_async_copy(buf.at[n, 0], (nw_a, nw_m)[j > 0].at[:, cols], new_sem.at[g, j])

    for g, j in ORDER:
        for copy in loads(g, j):
            copy.wait()
        buf, n, _ = chunk(g, j)
        scale = jnp.concatenate([ratio[0], ratio[1][0:4]], axis=0) if j == 0 else ratio[2][0:6]

        @pl.loop(0, STEPS)
        def _(step):
            def new(lo):
                cols = pl.ds(pl.multiple_of(lo * LANES + step * STEP, STEP), STEP)
                w, m, v = (buf[n, k, :, cols] for k in range(3))
                value = w - scale * direction(w, m, v)
                buf[n, 0, :, cols] = value
                return value

            pack_rows(j, new, lambda lo, value: put_cols(sbuf.at[g, j], lo, step, value.astype(BF16)))

        forward(g, 0, j, 0, sbuf.at[g, j])
        own_copy(g, j).start()
        new_copy(g, j).start()

    for step in (1, 2):
        for g, j in ORDER:
            forward(g, 0, j, step, sbuf.at[g, j])
    for g, j in ORDER:
        to_partner(g, 0, j, sbuf.at[g, j]).start()
    for rows, scale in zip(BLOCKS, ratio[3:]):
        nw_s[rows] = w_s[rows] - jnp.where(lane < HALF, scale, ratio[7]) * u_s[rows]
    small_buf[...] = nw_s[...].astype(BF16)
    spread(me, lambda peer: small_buf, small_full, t_send, t_recv)

    def receive(r, steps):
        for g, j in ORDER:
            arrival(g, r, j).wait_recv()
            for step in steps:
                forward(g, r, j, step)
            to_partner(g, r, j).start()

    receive(1, (1, 2))

    @pl.loop(2, 4)
    def _(r):
        receive(r, (2,))

    @pl.loop(4, 8)
    def _(r):
        receive(r, ())

    gather_wait(me, lambda peer: small_buf, small_full, t_send, t_recv)
    small_full[me] = small_buf[...]
    for g, j in ORDER:
        own_copy(g, j).wait()
        new_copy(g, j).wait()

    @pl.loop(0, 8)
    def _(r):
        for g, j in ORDER:
            to_partner(g, r, j).wait()

    @pl.loop(1, 8)
    def _(r):
        for g, j in ORDER:
            arrival(g, r, j).wait_send()


def gather_call(*args):
    hbm = pl.BlockSpec(memory_space=pl.ANY)
    vmem = pl.BlockSpec(memory_space=pltpu.VMEM)
    dma = pltpu.SemaphoreType.DMA
    sems = [dma((3, 8, 3))] * 4 + [dma((GROUPS, PARTS))] * 2 + [dma((3, 3, 3)), dma((6,))] + [dma((DEVICES,))] * 4
    return pl.pallas_call(
        gather_kernel,
        out_shape=[
            jax.ShapeDtypeStruct((DEVICES, GROUPS, PARTS, TILE, CHUNK), BF16),
            jax.ShapeDtypeStruct((DEVICES,) + SMALL, BF16),
            jax.ShapeDtypeStruct((A_ROWS, ATTN_W), F32),
            jax.ShapeDtypeStruct((M_ROWS, MLP_W), F32),
            jax.ShapeDtypeStruct(SMALL, F32),
        ],
        in_specs=[hbm] * len(args),
        out_specs=[hbm, vmem, hbm, hbm, vmem],
        scratch_shapes=[pltpu.VMEM(x.shape, F32) for x in args[6:]] + [
            pltpu.VMEM((GROUPS, PARTS, TILE, CHUNK), BF16),
            pltpu.VMEM((3, 3, A_ROWS, ATTN_COLS), F32),
            pltpu.VMEM((M_ROWS, 3, M_ROWS, MLP_COLS), F32),
            pltpu.VMEM((TILE, LANES), F32),
            pltpu.VMEM((DEVICES, TILE, LANES), F32),
            pltpu.VMEM(SMALL, BF16),
        ] + sems,
        compiler_params=pltpu.CompilerParams(collective_id=1, has_side_effects=True, vmem_limit_bytes=VMEM_LIMIT),
        name="all_gather",
    )(*args)


def unpack_moves(g, j, owner):
    if j == 0:
        start = owner * ATTN_W + g * ATTN_COLS
        moves = [(0, 8, 0, 2, 0, 0)] + [(4 * t, 4, 2, 1, 8, t) for t in range(2)]
    else:
        start = owner * MLP_W + (2 * g + j - 1) * MLP_COLS
        moves = [(0, 4, 0, 3, 0, 0), (4, 2, 0, 3, 4, 0)] + [(M_ROWS, 2, t, 1, 2 * t, 3) for t in range(3)]
    third = KT * LANES
    for row, rows, lo, width, to, at in moves:
        cols = pl.ds(pl.multiple_of(start + at * third, third), width * third)
        yield (pl.ds(row, rows), pl.ds(lo * third, width * third)), (pl.ds(to, rows), cols)


def unpack_kernel(full, small_full, nw_s, rep_a, rep_m, rep_vec, rep_wide, nw_vec, nw_wide, buf, load_sem, out_sem):
    sets = buf.shape[0]

    def loads(owner):
        return [pltpu.make_async_copy(full.at[owner, g, j], buf.at[lax.rem(owner, sets), g, j], load_sem.at[lax.rem(owner, sets), g, j]) for g, j in ORDER]

    def outs(owner, g, j):
        slot = lax.rem(owner, sets)
        rep = (rep_a, rep_m)[j > 0]
        return [pltpu.make_async_copy(buf.at[(slot, g, j) + src], rep.at[dst], out_sem.at[slot, g, j, n])
                for n, (src, dst) in enumerate(unpack_moves(g, j, owner))]

    def drain(owner):
        for g, j in ORDER:
            for copy in outs(owner, g, j):
                copy.wait()

    for owner in range(2):
        for copy in loads(owner):
            copy.start()

    @pl.loop(0, DEVICES)
    def _(owner):
        @pl.when(owner >= 2)
        def _():
            drain(owner - 2)

        @pl.when(owner < DEVICES - 2)
        def _():
            for copy in loads(owner + 2):
                copy.start()

        for (g, j), copy in zip(ORDER, loads(owner)):
            copy.wait()
            for move in outs(owner, g, j):
                move.start()

    vec = nw_vec.shape
    nw_vec[...] = nw_s[0:vec[0], 0:vec[1]]
    nw_wide[...] = jnp.concatenate(wide_pieces(nw_s), axis=1)
    shares = [small_full[n].astype(F32) for n in range(DEVICES)]
    rep_vec[...] = jnp.concatenate([x[0:vec[0], 0:vec[1]] for x in shares], axis=1).astype(BF16)
    rep_wide[...] = jnp.concatenate([piece for x in shares for piece in wide_pieces(x)], axis=1).astype(BF16)
    for owner in (DEVICES - 2, DEVICES - 1):
        drain(owner)


def unpack_call(full, small_full, nw_s):
    hbm = pl.BlockSpec(memory_space=pl.ANY)
    vmem = pl.BlockSpec(memory_space=pltpu.VMEM)
    return pl.pallas_call(
        unpack_kernel,
        in_specs=[hbm, vmem, vmem],
        out_specs=[hbm] * 2 + [vmem] * 4,
        out_shape=[
            jax.ShapeDtypeStruct((A_ROWS, DEVICES * ATTN_W), BF16),
            jax.ShapeDtypeStruct((M_ROWS, DEVICES * MLP_W), BF16),
            jax.ShapeDtypeStruct((29, 768), BF16),
            jax.ShapeDtypeStruct((3, 3072), BF16),
            jax.ShapeDtypeStruct((29, 48), F32),
            jax.ShapeDtypeStruct((3, 192), F32),
        ],
        scratch_shapes=[pltpu.VMEM((4, GROUPS, PARTS, TILE, CHUNK), BF16), pltpu.SemaphoreType.DMA((4, GROUPS, PARTS)), pltpu.SemaphoreType.DMA((4, GROUPS, PARTS, 5))],
        name="unpack",
    )(full, small_full, nw_s)


def solution(mesh):
    grad_spec = P("data", None, None)
    shard_spec = P(None, "data")
    full_spec = P(None, None)

    def local_step(*banks):
        grads, weights, firsts, seconds = (banks[n:n + 4] for n in range(0, len(banks), 4))
        by_wide, by_vec = (x[0].reshape(x.shape[1], DEVICES, -1) for x in grads[2:])
        by_wide = by_wide.reshape(GROUPS, DEVICES, GROUPS, HALF).transpose(1, 2, 0, 3)
        by_wide = jnp.pad(by_wide, ((0, 0), (0, 1), (0, TILE - GROUPS), (0, 0))).reshape(DEVICES, SMALL[0], HALF)
        by_vec = jnp.pad(by_vec.transpose(1, 0, 2), ((0, 0), (0, GROUPS), (0, HALF - by_vec.shape[2])))
        g_small = jnp.concatenate([by_vec, by_wide], axis=2)
        gs_a, gs_m, gs_s, clip = reduce_call(grads[0], grads[1], g_small)
        attn, mlp, wide, vec = zip(weights, firsts, seconds)
        outs = update_call((gs_a,) + attn, (gs_m,) + mlp, clip, gs_s, *vec, *wide)
        nm_a, nv_a, nm_m, nv_m, nm_vec, nv_vec, nm_wide, nv_wide = outs[:8]
        full, small_full, nw_a, nw_m, nw_s = gather_call(weights[0], nm_a, nv_a, weights[1], nm_m, nv_m, *outs[8:])
        rep_a, rep_m, rep_vec, rep_wide, nw_vec, nw_wide = unpack_call(full, small_full, nw_s)
        return (rep_a, rep_m, rep_wide, rep_vec, nw_a, nw_m, nw_wide, nw_vec,
                nm_a, nm_m, nm_wide, nm_vec, nv_a, nv_m, nv_wide, nv_vec)

    return jax.shard_map(local_step, mesh=mesh, in_specs=(grad_spec,) * 4 + (shard_spec,) * 12, out_specs=(full_spec,) * 4 + (shard_spec,) * 12, check_vma=False)
```

time: 1120 us -> 496 us (0.44)
  waiting for transfers between devices: 636 us -> 0 us
  Pallas kernels: 0 us -> 486 us
  blocking collectives: 304 us -> 0 us
  local copies, waits for them, and re-layouts: 77.2 us -> 7.33 us
  other arithmetic: 63.6 us -> 0.77 us
  between operations: 17.5 us -> 0.72 us
  starting transfers between devices: 16.2 us -> 0 us
    pallas_call x0 -> x4, Pallas kernels: none -> 486 us  [the longest x1 285 us: reduce_call(): pl.pallas_call(reduce_kernel, out_shape=[jax.ShapeDtypeStruct((A_ROWS, 8...]
    all_to_all x3 -> x0, waiting for transfers between devices: 441 us -> none  [local_step(): received = lax.all_to_all(by_owner, 'data', 1, 1, tiled=True)]
    all_to_all x1 -> x0, blocking collectives: 212 us -> none  [local_step(): received = lax.all_to_all(by_owner, 'data', 1, 1, tiled=True)]
    all_gather x2 -> x0, waiting for transfers between devices: 195 us -> none  [local_step(): lax.all_gather(new_weight.astype(jnp.bfloat16), 'data', axis=1, tiled=True)]
    psum x2 -> x0, blocking collectives: 65.7 us -> none  [the longest x1 33.1 us: local_step(): lax.psum(local_square, 'data')]
    unnamed x29 -> x5, local copies, waits for them, and re-layouts: 61.1 us -> 5.45 us
    reduce_sum x12 -> x0, other arithmetic: 47.6 us -> none  [the longest x4 25.4 us: local_step(): mean_grads.append(jnp.sum(received, axis=1, dtype=jnp.float32) / group_size)]
    all_gather x2 -> x0, blocking collectives: 26.3 us -> none  [local_step(): lax.all_gather(new_weight.astype(jnp.bfloat16), 'data', axis=1, tiled=True)]
  transfers between devices with their start and end apart: 5 -> 0, of which waited for: 4 -> 0; matrix products, arithmetic and copies ran while one was open for 5% -> 0% of each run, Pallas kernels for 0% -> 0%
where the time goes in v1:
time: 496 us; the launch traced here: 494 us
  Pallas kernels  486 us (98%)
  local copies, waits for them, and re-layouts  7.33 us (1%)
    pallas_call x1, Pallas kernels, reduce_call(): pl.pallas_call(reduce_kernel, out_shape=[jax.ShapeDtypeStruct((A_ROWS, 8...  285 us
    pallas_call x1, Pallas kernels, gather_call(): pl.pallas_call(gather_kernel, out_shape=[jax.ShapeDtypeStruct((DEVICES, G...  152 us
    pallas_call x1, Pallas kernels, unpack_call(): pl.pallas_call(unpack_kernel, in_specs=[hbm, vmem, vmem], out_specs=[hbm]...  31 us
    pallas_call x1, Pallas kernels, update_call(): pl.pallas_call(update_kernel, grid=(1,), in_specs=[hbm] * 8 + [whole(x.sh...  17.1 us

profile of v1, /device:TPU:0, one launch (start us, length us, event | category | flops | bytes accessed | tf_op | source)
XLA Modules:
  0.0 494.4 jit_solution(3254287419048769796)
XLA Ops:
  0.6 0.8 reshape_reshape_squeeze.3
  1.6 1.0 reshape_squeeze.3
  2.6 0.8 fusion.1.gsmall
  3.4 285.4 %reduce_scatter.1 = (bf16[12,294912]{1,0:T(8,128)(2,1)}, bf16[6,1179648]{1,0:T(8,128)(2,1)}, f32[12,36864]{1,0:T(8,128)}, f32[6,147456]{1,0:T(8,128)}, f32[32,128]{1,0:T(8,128)}, /*index=5*/f32[8,128]{1,0:T(8,128)}) custom-call(bf16[1,12,589824]{2,1,0:T(8,128)(2,1)} %ga.1, bf16[1,6,2359296]{2,1,0:T(8,128)(2,1)} %gm.1, bf16[16,32,128]{2,1,0:T(8,128)(2,1)} %fusion.1.gsmall), custom_call_target="tpu_custom_call" | custom-call | tf_op jit(solution)/shard_map/reduce_scatter/pallas_call | solution.py:300
  288.8 17.1 %update.1 = (f32[12,36864]{1,0:T(8,128)}, f32[12,36864]{1,0:T(8,128)}, f32[6,147456]{1,0:T(8,128)}, f32[6,147456]{1,0:T(8,128)}, f32[29,48]{1,0:T(8,128)}, /*ind...) custom-call(f32[12,36864]{1,0:T(8,128)} %get-tuple-element.45.refs_0, ...), custom_call_target="tpu_custom_call" | custom-call | tf_op jit(solution)/shard_map/update/pallas_call | solution.py:419
  305.9 152.1 %all_gather.1 = (bf16[16,3,3,8,18432]{4,3,2,1,0:T(8,128)(2,1)}, bf16[16,32,128]{2,1,0:T(8,128)(2,1)}, f32[12,36864]{1,0:T(8,128)}, f32[6,147456]{1,0:T(8,128)}, f32[32,128]{1,0:T(8,128)}) custom-call(f32[12,36864]{1,0:T(8,128)} %rest_0_.1, f32[12,36864]{1,0:T(8,128)} %get-tuple-element.98.rest_1_, f32[12,36864]{1,0:T(8,128)} %get-tuple-element.102.rest_2_, ...), custom_call_target="tpu_custom_call" | custom-call | tf_op jit(solution)/shard_map/all_gather/pallas_call | solution.py:580
  458.0 0.0 copy-start
  458.0 31.0 %unpack.1 = (bf16[12,589824]{1,0:T(8,128)(2,1)}, bf16[6,2359296]{1,0:T(8,128)(2,1)}, bf16[29,768]{1,0:T(8,128)(2,1)}, bf16[3,3072]{1,0:T(4,128)(2,1)}, f32[29,48]{1,0:T(8,128)}, /*index=5*/f32[3,192]{1,0:T(4,128)}) custom-call(bf16[16,3,3,8,18432]{4,3,2,1,0:T(8,128)(2,1)} %get-tuple-element.59.full, bf16[16,32,128]{2,1,0:T(8,128)(2,1)} %get-tuple-element.60.small_full, ...), custom_call_target="tpu_custom_call" | custom-call | tf_op jit(solution)/shard_map/unpack/pallas_call | solution.py:667
  489.0 0.0 copy-done
  489.0 1.4 copy.40
  490.4 4.0 copy.41
  (3 shorter events, 0.1 us)
Async XLA Ops:
  458.0 31.0 %copy-start = (f32[12,36864]{1,0:T(8,128)S(1)}, f32[12,36864]{1,0:T(8,128)}, u32[]{:S(2)}) copy-start(f32[12,36864]{1,0:T(8,128)} %get-tuple-element.94) | copy-start | bytes 5308420

commit v2 on v1

--- a/solution.py
+++ b/solution.py
@@ -34,13 +34,17 @@
 A_ROWS = 12
 M_ROWS = 6
 GROUPS = 3
+QUADS = 4
 PARTS = 3
 HALF = LANES // 2
 VMEM_LIMIT = 67043328
+LAST = 3
+ANTIPODE = 7
+FIRST_OWNERS = 10
 SMALL = (32, 128)
 WEIGHT = (1, 2, 4)
 BLOCKS = [slice(row, row + TILE) for row in range(0, SMALL[0], TILE)]
-ORDER = [(g, j) for j in range(3) for g in range(3)]
+ORDER = [(g, j) for j in range(GROUPS) for g in range(GROUPS)]
 AXES = ((0, 1, 2), (1, 2, 0), (2, 0, 1))
 
 
@@ -56,7 +60,7 @@
 
 def chip_at(bits, flips):
     total = 0
-    for axis in range(3):
+    for axis in range(GROUPS):
         total = total + flip(bits[axis], flips[axis]) * WEIGHT[axis]
     return total
 
@@ -114,12 +118,12 @@
 def pack_rows(part, load, put):
     if part == 0:
         a, b = load(0), load(KT)
-        put(0, a[0:8])
-        put(KT, b[0:8])
-        put(2 * KT, jnp.concatenate([a[8:12], b[8:12]], axis=0))
+        put(0, a[:TILE])
+        put(KT, b[:TILE])
+        put(2 * KT, jnp.concatenate([a[TILE:], b[TILE:]], axis=0))
     else:
         d = load(3 * KT)
-        for t in range(3):
+        for t in range(GROUPS):
             put(t * KT, jnp.concatenate([load(t * KT), d[2 * t:2 * t + 2]], axis=0))
 
 
@@ -308,10 +312,10 @@
             jax.ShapeDtypeStruct((TILE, LANES), F32),
         ],
         in_specs=[hbm, hbm, vmem],
-        out_specs=[hbm] * 4 + [vmem] * 2,
+        out_specs=[hbm] * QUADS + [vmem] * 2,
         scratch_shapes=[
-            pltpu.VMEM((GROUPS, 4, PARTS, TILE, CHUNK), F32),
-            pltpu.VMEM((GROUPS, 4, PARTS, TILE, CHUNK), F32),
+            pltpu.VMEM((GROUPS, QUADS, PARTS, TILE, CHUNK), F32),
+            pltpu.VMEM((GROUPS, QUADS, PARTS, TILE, CHUNK), F32),
             pltpu.VMEM((GROUPS, 2, PARTS, TILE, CHUNK), F32),
             pltpu.VMEM((GROUPS, PARTS, TILE, CHUNK), F32),
             pltpu.VMEM((2, 2, A_ROWS, ATTN_COLS), BF16),
@@ -319,8 +323,8 @@
             pltpu.VMEM((DEVICES,) + SMALL, BF16),
             pltpu.VMEM((DEVICES, TILE, LANES), F32),
             pltpu.VMEM((TILE, LANES), F32),
-            dma((2, 4, GROUPS, PARTS)), dma((2, 4, GROUPS, PARTS)),
-            dma((GROUPS, 4, PARTS)), dma((GROUPS, 4, PARTS)),
+            dma((2, QUADS, GROUPS, PARTS)), dma((2, QUADS, GROUPS, PARTS)),
+            dma((GROUPS, QUADS, PARTS)), dma((GROUPS, QUADS, PARTS)),
             dma((GROUPS, 2, PARTS)), dma((GROUPS, 2, PARTS)),
             dma((GROUPS, PARTS)), dma((GROUPS, PARTS)),
             dma((2, 2)), dma((GROUPS, PARTS, 5)),
@@ -371,7 +375,7 @@
     c = clip[0:1, 0:1]
     u_s[...] = jnp.zeros(SMALL, F32)
     w_s[...] = jnp.zeros(SMALL, F32)
-    grads = gs_s[0:vec[0].shape[0], 0:vec[0].shape[1]], jnp.concatenate(wide_pieces(gs_s), axis=1)
+    grads = gs_s[:vec[0].shape[0], :vec[0].shape[1]], jnp.concatenate(wide_pieces(gs_s), axis=1)
     for k, (grad, (w, m, v)) in enumerate(zip(grads, (vec, wide))):
         w = w[...]
         new = moments(grad, m[...], v[...], c)
@@ -379,7 +383,7 @@
             ref[...] = value
         for ref, value in ((u_s, direction(w, *new)), (w_s, w)):
             if k == 0:
-                ref[0:value.shape[0], 0:value.shape[1]] = value
+                ref[:value.shape[0], :value.shape[1]] = value
             else:
                 for t, rows in enumerate(BLOCKS[:GROUPS]):
                     ref[rows.start:rows.start + GROUPS, HALF:] = value[:, t * HALF:(t + 1) * HALF]
@@ -420,11 +424,11 @@
         update_kernel,
         grid=(1,),
         in_specs=[hbm] * 8 + [whole(x.shape) for x in small],
-        out_specs=[hbm] * 4 + [whole(shape) for shape in outs],
+        out_specs=[hbm] * QUADS + [whole(shape) for shape in outs],
         out_shape=[jax.ShapeDtypeStruct(shape, F32) for shape in [(A_ROWS, ATTN_W)] * 2 + [(M_ROWS, MLP_W)] * 2 + outs],
         scratch_shapes=[
-            pltpu.VMEM((GROUPS, 4, A_ROWS, ATTN_COLS), F32),
-            pltpu.VMEM((2 * GROUPS, 4, M_ROWS, MLP_COLS), F32),
+            pltpu.VMEM((GROUPS, QUADS, A_ROWS, ATTN_COLS), F32),
+            pltpu.VMEM((2 * GROUPS, QUADS, M_ROWS, MLP_COLS), F32),
             pltpu.SemaphoreType.DMA((GROUPS, PARTS, 4)),
             pltpu.SemaphoreType.DMA((GROUPS, PARTS, 2)),
         ],
@@ -435,10 +439,10 @@
 
 def gather_kernel(*rest):
     banks, rest = (rest[:3], rest[3:6]), rest[6:]
-    stats, (full, small_full, nw_a, nw_m, nw_s) = rest[:6], rest[6:11]
-    stat_bufs, rest = rest[11:17], rest[17:]
-    (sbuf, st_a, st_m, tile, slots, small_buf, x_send, x_recv, d_send, d_recv,
-     own_sem, new_sem, load_sem, stat_sem, n_send, n_recv, t_send, t_recv) = rest
+    stats, (full, small_full, nw_a, nw_m, nw_s) = rest[:6], rest[9:14]
+    last, stat_bufs, rest = rest[6:9], rest[14:20], rest[20:]
+    (sbuf, keep, st_a, st_m, tile, slots, small_buf, x_send, x_recv, d_send, d_recv,
+     own_sem, new_sem, keep_in, keep_out, load_sem, stat_sem, n_send, n_recv, t_send, t_recv) = rest
     u_s, w_s, uu_a, ww_a, uu_m, ww_m = stat_bufs
     me, core, bits = position()
     partner = me + 1 - 2 * core
@@ -470,7 +474,7 @@
         a, m, s = a[...], m[...], s[...] * s[...]
         vec = jnp.where(lax.broadcasted_iota(jnp.int32, SMALL, 1) < HALF, s, 0.0)
         wide = s - vec
-        blocks = [a[0:TILE], pad8(a[TILE:]), pad8(m)] + [vec[rows] for rows in BLOCKS] + [sum(wide[rows] for rows in BLOCKS)]
+        blocks = [a[:TILE], pad8(a[TILE:]), pad8(m)] + [vec[rows] for rows in BLOCKS] + [sum(wide[rows] for rows in BLOCKS)]
         for l, block in enumerate(blocks):
             out = jnp.where(lane == TILE * k + l, jnp.sum(block, axis=1, keepdims=True), out)
     tile[...] = out
@@ -484,21 +488,29 @@
         owner = 2 * chip_at(bits, flips_of(g, lax.rem(r, 2), lax.rem(r // 2, 2), r // 4)) + core
         return full.at[owner, g, j]
 
-    def copy_to(g, r, j, to, arrived, sends, recvs, src):
+    def landing(g, r, j, arrived):
+        return last[g].at[j] if arrived is LAST else place(g, r, j)
+
+    def keep_copies(g, j):
+        return (pltpu.make_async_copy(last[g].at[j], keep.at[g, j], keep_in.at[g, j]),
+                pltpu.make_async_copy(keep.at[g, j], place(g, LAST, j), keep_out.at[g, j]))
+
+    def copy_to(g, r, j, to, arrived, sends, recvs, src, dst=None):
         return pltpu.make_async_remote_copy(
-            src_ref=src, dst_ref=place(g, r, j), send_sem=sends.at[g, arrived, j], recv_sem=recvs.at[g, arrived, j],
+            src_ref=src, dst_ref=place(g, r, j) if dst is None else dst, send_sem=sends.at[g, arrived, j], recv_sem=recvs.at[g, arrived, j],
             device_id=(to,), device_id_type=MESH)
 
     def forward(g, r, j, step, src=None):
         axis = AXES[g][step]
         to = me + WEIGHT[axis] * 2 * (1 - 2 * bits[axis])
-        copy_to(g, r, j, to, r + WEIGHT[step], x_send, x_recv, place(g, r, j) if src is None else src).start()
+        arrived = r + WEIGHT[step]
+        copy_to(g, r, j, to, arrived, x_send, x_recv, place(g, r, j) if src is None else src, landing(g, r, j, arrived)).start()
 
     def to_partner(g, r, j, src=None):
         return copy_to(g, r, j, partner, r, d_send, d_recv, place(g, r, j) if src is None else src)
 
     def arrival(g, r, j):
-        return copy_to(g, r, j, partner, r, x_send, x_recv, place(g, r, j))
+        return copy_to(g, r, j, partner, r, x_send, x_recv, place(g, r, j), landing(g, r, j, r))
 
     def own_copy(g, j):
         return pltpu.make_async_copy(sbuf.at[g, j], place(g, 0, j), own_sem.at[g, j])
@@ -517,7 +529,7 @@
         def _(step):
             def new(lo):
                 cols = pl.ds(pl.multiple_of(lo * LANES + step * STEP, STEP), STEP)
-                w, m, v = (buf[n, k, :, cols] for k in range(3))
+                w, m, v = (buf[n, k, :, cols] for k in range(GROUPS))
                 value = w - scale * direction(w, m, v)
                 buf[n, 0, :, cols] = value
                 return value
@@ -543,30 +555,36 @@
             arrival(g, r, j).wait_recv()
             for step in steps:
                 forward(g, r, j, step)
-            to_partner(g, r, j).start()
+            to_partner(g, r, j, landing(g, r, j, r)).start()
+            if r is LAST:
+                keep_copies(g, j)[0].start()
 
     receive(1, (1, 2))
-
-    @pl.loop(2, 4)
-    def _(r):
-        receive(r, (2,))
-
-    @pl.loop(4, 8)
+    receive(2, (2,))
+    receive(LAST, ())
+
+    @pl.loop(LAST + 1, ANTIPODE)
     def _(r):
         receive(r, ())
 
+    for g, j in ORDER:
+        into, out_of = keep_copies(g, j)
+        into.wait()
+        out_of.start()
+
     gather_wait(me, lambda peer: small_buf, small_full, t_send, t_recv)
     small_full[me] = small_buf[...]
     for g, j in ORDER:
         own_copy(g, j).wait()
+        keep_copies(g, j)[1].wait()
         new_copy(g, j).wait()
 
-    @pl.loop(0, 8)
+    @pl.loop(0, ANTIPODE)
     def _(r):
         for g, j in ORDER:
             to_partner(g, r, j).wait()
 
-    @pl.loop(1, 8)
+    @pl.loop(1, ANTIPODE)
     def _(r):
         for g, j in ORDER:
             arrival(g, r, j).wait_send()
@@ -576,10 +594,10 @@
     hbm = pl.BlockSpec(memory_space=pl.ANY)
     vmem = pl.BlockSpec(memory_space=pltpu.VMEM)
     dma = pltpu.SemaphoreType.DMA
-    sems = [dma((3, 8, 3))] * 4 + [dma((GROUPS, PARTS))] * 2 + [dma((3, 3, 3)), dma((6,))] + [dma((DEVICES,))] * 4
+    sems = [dma((GROUPS, TILE, PARTS))] * 4 + [dma((GROUPS, PARTS))] * 4 + [dma((GROUPS, PARTS, GROUPS)), dma((6,))] + [dma((DEVICES,))] * 4
     return pl.pallas_call(
         gather_kernel,
-        out_shape=[
+        out_shape=[jax.ShapeDtypeStruct((PARTS, TILE, CHUNK), BF16)] * GROUPS + [
             jax.ShapeDtypeStruct((DEVICES, GROUPS, PARTS, TILE, CHUNK), BF16),
             jax.ShapeDtypeStruct((DEVICES,) + SMALL, BF16),
             jax.ShapeDtypeStruct((A_ROWS, ATTN_W), F32),
@@ -587,8 +605,9 @@
             jax.ShapeDtypeStruct(SMALL, F32),
         ],
         in_specs=[hbm] * len(args),
-        out_specs=[hbm, vmem, hbm, hbm, vmem],
+        out_specs=[hbm] * (GROUPS + 1) + [vmem, hbm, hbm, vmem],
         scratch_shapes=[pltpu.VMEM(x.shape, F32) for x in args[6:]] + [
+            pltpu.VMEM((GROUPS, PARTS, TILE, CHUNK), BF16),
             pltpu.VMEM((GROUPS, PARTS, TILE, CHUNK), BF16),
             pltpu.VMEM((3, 3, A_ROWS, ATTN_COLS), F32),
             pltpu.VMEM((M_ROWS, 3, M_ROWS, MLP_COLS), F32),
@@ -607,78 +626,103 @@
         moves = [(0, 8, 0, 2, 0, 0)] + [(4 * t, 4, 2, 1, 8, t) for t in range(2)]
     else:
         start = owner * MLP_W + (2 * g + j - 1) * MLP_COLS
-        moves = [(0, 4, 0, 3, 0, 0), (4, 2, 0, 3, 4, 0)] + [(M_ROWS, 2, t, 1, 2 * t, 3) for t in range(3)]
+        moves = [(0, 4, 0, 3, 0, 0), (4, 2, 0, 3, 4, 0)] + [(M_ROWS, 2, t, 1, 2 * t, 3) for t in range(GROUPS)]
     third = KT * LANES
     for row, rows, lo, width, to, at in moves:
         cols = pl.ds(pl.multiple_of(start + at * third, third), width * third)
         yield (pl.ds(row, rows), pl.ds(lo * third, width * third)), (pl.ds(to, rows), cols)
 
 
-def unpack_kernel(full, small_full, nw_s, rep_a, rep_m, rep_vec, rep_wide, nw_vec, nw_wide, buf, load_sem, out_sem):
-    sets = buf.shape[0]
-
-    def loads(owner):
-        return [pltpu.make_async_copy(full.at[owner, g, j], buf.at[lax.rem(owner, sets), g, j], load_sem.at[lax.rem(owner, sets), g, j]) for g, j in ORDER]
-
-    def outs(owner, g, j):
-        slot = lax.rem(owner, sets)
-        rep = (rep_a, rep_m)[j > 0]
-        return [pltpu.make_async_copy(buf.at[(slot, g, j) + src], rep.at[dst], out_sem.at[slot, g, j, n])
-                for n, (src, dst) in enumerate(unpack_moves(g, j, owner))]
-
-    def drain(owner):
+def stream(count, owner_of, source, reps, buf, load_sem, out_sem):
+    def loads(t):
+        slot = lax.rem(t, buf.shape[0])
+        return [pltpu.make_async_copy(source(t, g, j), buf.at[slot, g, j], load_sem.at[slot, g, j]) for g, j in ORDER]
+
+    def outs(t, g, j):
+        slot = lax.rem(t, buf.shape[0])
+        return [pltpu.make_async_copy(buf.at[(slot, g, j) + src], reps[j > 0].at[dst], out_sem.at[slot, g, j, n])
+                for n, (src, dst) in enumerate(unpack_moves(g, j, owner_of(t)))]
+
+    def begin(t):
+        for copy in loads(t):
+            copy.start()
+
+    def move(t):
+        for (g, j), copy in zip(ORDER, loads(t)):
+            copy.wait()
+            for out in outs(t, g, j):
+                out.start()
+
+    def drain(t):
         for g, j in ORDER:
-            for copy in outs(owner, g, j):
-                copy.wait()
-
-    for owner in range(2):
-        for copy in loads(owner):
-            copy.start()
-
-    @pl.loop(0, DEVICES)
-    def _(owner):
-        @pl.when(owner >= 2)
-        def _():
-            drain(owner - 2)
-
-        @pl.when(owner < DEVICES - 2)
-        def _():
-            for copy in loads(owner + 2):
-                copy.start()
-
-        for (g, j), copy in zip(ORDER, loads(owner)):
-            copy.wait()
-            for move in outs(owner, g, j):
-                move.start()
-
+            for out in outs(t, g, j):
+                out.wait()
+
+    begin(0)
+    begin(1)
+    if count > 2:
+        @pl.loop(0, count)
+        def _(t):
+            pl.when(t >= 2)(lambda: drain(t - 2))
+            pl.when(t < count - 2)(lambda: begin(t + 2))
+            move(t)
+    else:
+        move(0)
+        move(1)
+    drain(count - 2)
+    drain(count - 1)
+
+
+def far_owner(skip):
+    _, core, bits = position()
+    far = 2 * chip_at(bits, (1, 1, 1))
+    return lambda t: lax.rem(far + skip + t, DEVICES), far, core
+
+
+def unpack_kernel(full, small_full, nw_s, rep_a, rep_m, rep_vec, rep_wide, nw_vec, nw_wide, *scratch):
+    owner_of = far_owner(2)[0]
+    stream(FIRST_OWNERS, owner_of, lambda t, g, j: full.at[owner_of(t), g, j], (rep_a, rep_m), *scratch)
     vec = nw_vec.shape
-    nw_vec[...] = nw_s[0:vec[0], 0:vec[1]]
+    nw_vec[...] = nw_s[:vec[0], :vec[1]]
     nw_wide[...] = jnp.concatenate(wide_pieces(nw_s), axis=1)
     shares = [small_full[n].astype(F32) for n in range(DEVICES)]
-    rep_vec[...] = jnp.concatenate([x[0:vec[0], 0:vec[1]] for x in shares], axis=1).astype(BF16)
+    rep_vec[...] = jnp.concatenate([x[:vec[0], :vec[1]] for x in shares], axis=1).astype(BF16)
     rep_wide[...] = jnp.concatenate([piece for x in shares for piece in wide_pieces(x)], axis=1).astype(BF16)
-    for owner in (DEVICES - 2, DEVICES - 1):
-        drain(owner)
-
-
-def unpack_call(full, small_full, nw_s):
+
+
+def more_kernel(full, *refs):
+    owner_of = far_owner(2 + FIRST_OWNERS)[0]
+    stream(DEVICES - 2 - FIRST_OWNERS, owner_of, lambda t, g, j: full.at[owner_of(t), g, j], refs[-5:-3], *refs[-3:])
+
+
+def far_kernel(*refs):
+    _, far, core = far_owner(0)
+    stream(2, lambda t: far + flip(core, t), lambda t, g, j: refs[t * GROUPS + g].at[j], refs[-5:-3], *refs[-3:])
+
+
+REPLICAS = [jax.ShapeDtypeStruct((A_ROWS, DEVICES * ATTN_W), BF16), jax.ShapeDtypeStruct((M_ROWS, DEVICES * MLP_W), BF16)]
+
+
+def stream_call(kernel, name, ins, vmem_ins=(), vmem_outs=(), reps=()):
     hbm = pl.BlockSpec(memory_space=pl.ANY)
     vmem = pl.BlockSpec(memory_space=pltpu.VMEM)
+    dma = pltpu.SemaphoreType.DMA
+    count = len(ins) + len(vmem_ins)
     return pl.pallas_call(
-        unpack_kernel,
-        in_specs=[hbm, vmem, vmem],
-        out_specs=[hbm] * 2 + [vmem] * 4,
-        out_shape=[
-            jax.ShapeDtypeStruct((A_ROWS, DEVICES * ATTN_W), BF16),
-            jax.ShapeDtypeStruct((M_ROWS, DEVICES * MLP_W), BF16),
-            jax.ShapeDtypeStruct((29, 768), BF16),
-            jax.ShapeDtypeStruct((3, 3072), BF16),
-            jax.ShapeDtypeStruct((29, 48), F32),
-            jax.ShapeDtypeStruct((3, 192), F32),
-        ],
-        scratch_shapes=[pltpu.VMEM((4, GROUPS, PARTS, TILE, CHUNK), BF16), pltpu.SemaphoreType.DMA((4, GROUPS, PARTS)), pltpu.SemaphoreType.DMA((4, GROUPS, PARTS, 5))],
-        name="unpack",
-    )(full, small_full, nw_s)
+        kernel,
+        in_specs=[hbm] * len(ins) + [vmem] * len(vmem_ins) + [hbm] * len(reps),
+        out_specs=[hbm] * 2 + [vmem] * len(vmem_outs),
+        out_shape=REPLICAS + list(vmem_outs),
+        scratch_shapes=[pltpu.VMEM((QUADS, GROUPS, PARTS, TILE, CHUNK), BF16), dma((QUADS, GROUPS, PARTS)), dma((QUADS, GROUPS, PARTS, 5))],
+        input_output_aliases={count + n: n for n in range(len(reps))},
+        cost_estimate=pl.CostEstimate(flops=10 ** 9, bytes_accessed=2 ** 26, transcendentals=0),
+        compiler_params=pltpu.CompilerParams(vmem_limit_bytes=VMEM_LIMIT),
+        name=name,
+    )(*ins, *vmem_ins, *reps)
+
+
+def swap(x, weight):
+    return lax.ppermute(x, "data", [(d, d ^ weight) for d in range(DEVICES)])
 
 
 def solution(mesh):
@@ -697,8 +741,15 @@
         attn, mlp, wide, vec = zip(weights, firsts, seconds)
         outs = update_call((gs_a,) + attn, (gs_m,) + mlp, clip, gs_s, *vec, *wide)
         nm_a, nv_a, nm_m, nv_m, nm_vec, nv_vec, nm_wide, nv_wide = outs[:8]
-        full, small_full, nw_a, nw_m, nw_s = gather_call(weights[0], nm_a, nv_a, weights[1], nm_m, nv_m, *outs[8:])
-        rep_a, rep_m, rep_vec, rep_wide, nw_vec, nw_wide = unpack_call(full, small_full, nw_s)
+        outs = gather_call(weights[0], nm_a, nv_a, weights[1], nm_m, nv_m, *outs[8:])
+        last, (full, small_full, nw_a, nw_m, nw_s) = outs[:GROUPS], outs[GROUPS:]
+        far = [swap(x, 2 * WEIGHT[axes[2]]) for x, axes in zip(last, AXES)]
+        tail = [jax.ShapeDtypeStruct(shape, dtype) for dtype, bank in ((BF16, grads), (F32, weights)) for shape in (bank[3].shape[-2:], bank[2].shape[-2:])]
+        rep_a, rep_m, rep_vec, rep_wide, nw_vec, nw_wide = stream_call(unpack_kernel, "unpack", [full], (small_full, nw_s), tail)
+        far, rep_a, rep_m = lax.optimization_barrier((far, rep_a, rep_m))
+        across = [swap(x, 1) for x in far]
+        reps = stream_call(more_kernel, "unpack_more", [full] + far, reps=(rep_a, rep_m))
+        rep_a, rep_m = stream_call(far_kernel, "unpack_far", far + across, reps=reps)
         return (rep_a, rep_m, rep_wide, rep_vec, nw_a, nw_m, nw_wide, nw_vec,
                 nm_a, nm_m, nm_wide, nm_vec, nv_a, nv_m, nv_wide, nv_vec)
 

time: 496 us -> 490 us (0.988)
  Pallas kernels: 486 us -> 473 us
    pallas_call x2 -> x4, Pallas kernels: 183 us -> 170 us  [the longest x1 133 us: gather_call(): pl.pallas_call(gather_kernel, out_shape=[jax.ShapeDtypeStruct((PARTS, TIL...]
  transfers between devices with their start and end apart: 0 -> 6, of which waited for: 0 -> 0; matrix products, arithmetic and copies ran while one was open for 0% -> 0% of each run, Pallas kernels for 0% -> 6%
where the time goes in v2:
time: 490 us; the launch traced here: 489 us
  Pallas kernels  473 us (97%)
  local copies, waits for them, and re-layouts  9.14 us (2%)
  starting transfers between devices  4.94 us (1%)
    pallas_call x1, Pallas kernels, reduce_call(): pl.pallas_call(reduce_kernel, out_shape=[jax.ShapeDtypeStruct((A_ROWS, 8...  285 us
    pallas_call x1, Pallas kernels, gather_call(): pl.pallas_call(gather_kernel, out_shape=[jax.ShapeDtypeStruct((PARTS, TIL...  133 us
    pallas_call x3, Pallas kernels, stream_call(): pl.pallas_call(kernel, in_specs=[hbm] * len(ins) + [vmem] * len(vmem_ins)...  37.2 us
    pallas_call x1, Pallas kernels, update_call(): pl.pallas_call(update_kernel, grid=(1,), in_specs=[hbm] * 8 + [whole(x.sh...  17.1 us
  transfers between devices with their start and end apart: 6, of which 0 were waited for; matrix products, arithmetic and copies ran while one was open for 0% of the time, Pallas kernels for 6%

profile of v2, /device:TPU:0, one launch (start us, length us, event | category | flops | bytes accessed | tf_op | source)
XLA Modules:
  0.0 488.7 jit_solution(18088809061401956049)
XLA Ops:
  0.6 0.8 reshape_reshape_squeeze.3
  1.6 1.0 reshape_squeeze.3
  2.6 0.8 fusion.1.gsmall
  3.4 285.4 %reduce_scatter.1 = (bf16[12,294912]{1,0:T(8,128)(2,1)}, bf16[6,1179648]{1,0:T(8,128)(2,1)}, f32[12,36864]{1,0:T(8,128)}, f32[6,147456]{1,0:T(8,128)}, f32[32,128]{1,0:T(8,128)}, /*index=5*/f32[8,128]{1,0:T(8,128)}) custom-call(bf16[1,12,589824]{2,1,0:T(8,128)(2,1)} %ga.1, bf16[1,6,2359296]{2,1,0:T(8,128)(2,1)} %gm.1, bf16[16,32,128]{2,1,0:T(8,128)(2,1)} %fusion.1.gsmall), custom_call_target="tpu_custom_call" | custom-call | tf_op jit(solution)/shard_map/reduce_scatter/pallas_call | solution.py:304
  288.7 17.1 %update.1 = (f32[12,36864]{1,0:T(8,128)}, f32[12,36864]{1,0:T(8,128)}, f32[6,147456]{1,0:T(8,128)}, f32[6,147456]{1,0:T(8,128)}, f32[29,48]{1,0:T(8,128)}, /*ind...) custom-call(f32[12,36864]{1,0:T(8,128)} %get-tuple-element.57.refs_0, ...), custom_call_target="tpu_custom_call" | custom-call | tf_op jit(solution)/shard_map/update/pallas_call | solution.py:423
  305.9 133.3 %all_gather.1 = (bf16[3,8,18432]{2,1,0:T(8,128)(2,1)}, bf16[3,8,18432]{2,1,0:T(8,128)(2,1)}, bf16[3,8,18432]{2,1,0:T(8,128)(2,1)}, bf16[16,3,3,8,18432]{4,3,2,1,...) custom-call(f32[12,36864]{1,0:T(8,128)} %rest_0_.1, ...), custom_call_target="tpu_custom_call" | custom-call | tf_op jit(solution)/shard_map/all_gather/pallas_call | solution.py:598
  439.2 1.3 collective-permute-start
  440.5 1.5 collective-permute-start.1
  442.0 1.5 collective-permute-start.2
  443.5 21.1 %unpack.1 = (bf16[12,589824]{1,0:T(8,128)(2,1)}, bf16[6,2359296]{1,0:T(8,128)(2,1)}, bf16[29,768]{1,0:T(8,128)(2,1)}, bf16[3,3072]{1,0:T(4,128)(2,1)}, f32[29,48]{1,0:T(8,128)}, /*index=5*/f32[3,192]{1,0:T(4,128)}) custom-call(bf16[16,3,3,8,18432]{4,3,2,1,0:T(8,128)(2,1)} %get-tuple-element.74.full, bf16[16,32,128]{2,1,0:T(8,128)(2,1)} %get-tuple-element.75.small_full, ...), custom_call_target="tpu_custom_call" | custom-call | flops 1000000000 | bytes 67108864 | tf_op jit(solution)/shard_map/unpack/pallas_call | solution.py:711
  464.6 0.0 collective-permute-done.refs_0_
  464.6 0.0 collective-permute-done.1.refs_1_
  464.6 0.0 collective-permute-done.2.refs_2_
  464.6 0.0 collective-permute-start.3
  464.7 0.5 collective-permute-start.4
  465.2 0.1 collective-permute-start.5
  465.2 9.6 %unpack_more.1 = (bf16[12,589824]{1,0:T(8,128)(2,1)}, bf16[6,2359296]{1,0:T(8,128)(2,1)}) custom-call(bf16[16,3,3,8,18432]{4,3,2,1,0:T(8,128)(2,1)} %get-tuple-element.74.full, bf16[3,8,18432]{2,1,0:T(8,128)(2,1)} %collective-permute-done.refs_0_, bf16[3,8,18432]{2,1,0:T(8,128)(2,1)} %collective-permute-done.1.refs_1_, ...), custom_call_target="tpu_custom_call", output_to_operand_aliasing={{0}: (4, {}), {1}: (5, {})} | custom-call | flops 1000000000 | bytes 67108864 | tf_op jit(solution)/shard_map/unpack_more/pallas_call | solution.py:711
  474.8 0.0 collective-permute-done.3.refs_3_
  474.8 0.0 collective-permute-done.4.refs_4_
  474.8 0.0 collective-permute-done.5.refs_5_
  474.8 6.6 %unpack_far.1 = (bf16[12,589824]{1,0:T(8,128)(2,1)}, bf16[6,2359296]{1,0:T(8,128)(2,1)}) custom-call(bf16[3,8,18432]{2,1,0:T(8,128)(2,1)} %collective-permute-done.refs_0_, bf16[3,8,18432]{2,1,0:T(8,128)(2,1)} %collective-permute-done.1.refs_1_, bf16[3,8,18432]{2,1,0:T(8,128)(2,1)} %collective-permute-done.2.refs_2_, ...), custom_call_target="tpu_custom_call", output_to_operand_aliasing={{0}: (6, {}), {1}: (7, {})} | custom-call | flops 1000000000 | bytes 67108864 | tf_op jit(solution)/shard_map/unpack_far/pallas_call | solution.py:711
  481.4 3.2 copy.48
  484.7 4.0 copy.49
  (3 shorter events, 0.1 us)
Async XLA Ops:
  439.2 25.4 %collective-permute-start = (bf16[3,8,18432]{2,1,0:T(8,128)(2,1)}, bf16[3,8,18432]{2,1,0:T(8,128)(2,1)}, u32[]{:S(2)}, u32[]{:S(2)}) collective-permute-start(bf16[3,8,18432]{2,1,0:T(8,128)(2,1)} %get-tuple-element.71), channel_id=1, source_target_pairs={{0,8},{1,9},{2,10},{3,11},{4,12},{5,13},{6,14},{7,15},{8,0},{9,1},... | collective-permute-start | bytes 2654216 | tf_op jit(solution)/shard_map/ppermute | solution.py:725
  440.5 24.1 %collective-permute-start.1 = (bf16[3,8,18432]{2,1,0:T(8,128)(2,1)}, bf16[3,8,18432]{2,1,0:T(8,128)(2,1)}, u32[]{:S(2)}, u32[]{:S(2)}) collective-permute-start(bf16[3,8,18432]{2,1,0:T(8,128)(2,1)} %get-tuple-element.72), channel_id=1, source_target_pairs={{0,2},{1,3},{2,0},{3,1},{4,6},{5,7},{6,4},{7,5},{8,10},{9,11},{10,... | collective-permute-start | bytes 2654216 | tf_op jit(solution)/shard_map/ppermute | solution.py:725
  442.0 22.6 %collective-permute-start.2 = (bf16[3,8,18432]{2,1,0:T(8,128)(2,1)}, bf16[3,8,18432]{2,1,0:T(8,128)(2,1)}, u32[]{:S(2)}, u32[]{:S(2)}) collective-permute-start(bf16[3,8,18432]{2,1,0:T(8,128)(2,1)} %get-tuple-element.73), channel_id=1, source_target_pairs={{0,4},{1,5},{2,6},{3,7},{4,0},{5,1},{6,2},{7,3},{8,12},{9,13},{10,... | collective-permute-start | bytes 2654216 | tf_op jit(solution)/shard_map/ppermute | solution.py:725
  464.6 10.2 %collective-permute-start.3 = (bf16[3,8,18432]{2,1,0:T(8,128)(2,1)}, bf16[3,8,18432]{2,1,0:T(8,128)(2,1)}, u32[]{:S(2)}, u32[]{:S(2)}) collective-permute-start(bf16[3,8,18432]{2,1,0:T(8,128)(2,1)} %collective-permute-done.refs_0_), channel_id=1, source_target_pairs={{0,1},{1,0},{2,3},{3,2},{4,5},{5,4},{6,7},{7,6},{8,9},{9,8},{10,11... | collective-permute-start | bytes 2654216 | tf_op jit(solution)/shard_map/ppermute | solution.py:725
  464.7 10.2 %collective-permute-start.4 = (bf16[3,8,18432]{2,1,0:T(8,128)(2,1)}, bf16[3,8,18432]{2,1,0:T(8,128)(2,1)}, u32[]{:S(2)}, u32[]{:S(2)}) collective-permute-start(bf16[3,8,18432]{2,1,0:T(8,128)(2,1)} %collective-permute-done.1.refs_1_), channel_id=1, source_target_pairs={{0,1},{1,0},{2,3},{3,2},{4,5},{5,4},{6,7},{7,6},{8,9},{9,8},{10,11... | collective-permute-start | bytes 2654216 | tf_op jit(solution)/shard_map/ppermute | solution.py:725
  465.2 9.7 %collective-permute-start.5 = (bf16[3,8,18432]{2,1,0:T(8,128)(2,1)}, bf16[3,8,18432]{2,1,0:T(8,128)(2,1)}, u32[]{:S(2)}, u32[]{:S(2)}) collective-permute-start(bf16[3,8,18432]{2,1,0:T(8,128)(2,1)} %collective-permute-done.2.refs_2_), channel_id=1, source_target_pairs={{0,1},{1,0},{2,3},{3,2},{4,5},{5,4},{6,7},{7,6},{8,9},{9,8},{10,11... | collective-permute-start | bytes 2654216 | tf_op jit(solution)/shard_map/ppermute | solution.py:725

commit v3 on v2

--- a/solution.py
+++ b/solution.py
@@ -145,11 +145,14 @@
     return sum(x[:, l:l + LANES] for l in range(0, x.shape[1], LANES))
 
 
-def reduce_kernel(ga, gm, gsmall, pa, pm, gs_a, gs_m, small_out, clip_out,
-                  sbuf, r1, r2, r3, raw_a, raw_m, small_slots, norm_slots, acc,
-                  d_send, d_recv, s1, q1, s2, q2, s3, q3, load_sem, out_sem, t_send, t_recv, n_send, n_recv):
+def reduce_kernel(ga, gm, gvec, gwide, pa, pm, gs_a, gs_m, small_out, clip_out,
+                  sbuf, r1, r2, r3, raw_a, raw_m, raw_vec, raw_wide, block, gsmall, small_slots, norm_slots, acc,
+                  d_send, d_recv, s1, q1, s2, q2, s3, q3, load_sem, out_sem, t_send, t_recv, n_send, n_recv, v_sem):
     me, core, bits = position()
     partner = me + 1 - 2 * core
+    small_loads = [pltpu.make_async_copy(src.at[0], dst, v_sem.at[n]) for n, (src, dst) in enumerate(((gvec, raw_vec), (gwide, raw_wide)))]
+    for copy in small_loads:
+        copy.start()
     signal_all(me)
 
     def neighbour(axis):
@@ -172,8 +175,6 @@
         def _(i):
             for g, j in ORDER:
                 pair_copy(half, i, g, j).start()
-        if half == 0:
-            spread(me, lambda peer: gsmall.at[peer], small_slots, t_send, t_recv)
 
     def loads(half, i, g, j, slot):
         chip = owner_chip(half, i, g)
@@ -219,6 +220,19 @@
     def _(i):
         sweep(0, i, first)
 
+    for copy in small_loads:
+        copy.wait()
+    vec, wide = raw_vec[...].astype(F32), raw_wide[...].astype(F32)
+    share = vec.shape[1] // DEVICES
+    block[...] = jnp.zeros(SMALL, F32)
+    for owner in range(DEVICES):
+        block[:vec.shape[0], :share] = vec[:, owner * share:(owner + 1) * share]
+        for t, rows in enumerate(BLOCKS[:GROUPS]):
+            lane = (owner * GROUPS + t) * HALF
+            block[rows.start:rows.start + GROUPS, HALF:] = wide[:, lane:lane + HALF]
+        gsmall[owner] = block[...].astype(BF16)
+    spread(me, lambda peer: gsmall.at[peer], small_slots, t_send, t_recv)
+
     def second(i, g, j, own, par):
         send1(i, g, j).wait_recv()
         pack_sum(j, own, par, r1.at[g, i, j], r1.at[g, i, j])
@@ -297,7 +311,7 @@
             pair_copy(1, i, g, j).wait_send()
 
 
-def reduce_call(ga, gm, gsmall):
+def reduce_call(*grads):
     hbm = pl.BlockSpec(memory_space=pl.ANY)
     vmem = pl.BlockSpec(memory_space=pltpu.VMEM)
     dma = pltpu.SemaphoreType.DMA
@@ -311,7 +325,7 @@
             jax.ShapeDtypeStruct(SMALL, F32),
             jax.ShapeDtypeStruct((TILE, LANES), F32),
         ],
-        in_specs=[hbm, hbm, vmem],
+        in_specs=[hbm] * QUADS,
         out_specs=[hbm] * QUADS + [vmem] * 2,
         scratch_shapes=[
             pltpu.VMEM((GROUPS, QUADS, PARTS, TILE, CHUNK), F32),
@@ -320,6 +334,10 @@
             pltpu.VMEM((GROUPS, PARTS, TILE, CHUNK), F32),
             pltpu.VMEM((2, 2, A_ROWS, ATTN_COLS), BF16),
             pltpu.VMEM((2, 2, M_ROWS, MLP_COLS), BF16),
+            pltpu.VMEM(grads[2].shape[1:], BF16),
+            pltpu.VMEM(grads[3].shape[1:], BF16),
+            pltpu.VMEM(SMALL, F32),
+            pltpu.VMEM((DEVICES,) + SMALL, BF16),
             pltpu.VMEM((DEVICES,) + SMALL, BF16),
             pltpu.VMEM((DEVICES, TILE, LANES), F32),
             pltpu.VMEM((TILE, LANES), F32),
@@ -328,11 +346,11 @@
             dma((GROUPS, 2, PARTS)), dma((GROUPS, 2, PARTS)),
             dma((GROUPS, PARTS)), dma((GROUPS, PARTS)),
             dma((2, 2)), dma((GROUPS, PARTS, 5)),
-            dma((DEVICES,)), dma((DEVICES,)), dma((DEVICES,)), dma((DEVICES,)),
+            dma((DEVICES,)), dma((DEVICES,)), dma((DEVICES,)), dma((DEVICES,)), dma((2,)),
         ],
         compiler_params=pltpu.CompilerParams(collective_id=0, has_side_effects=True, vmem_limit_bytes=VMEM_LIMIT),
         name="reduce_scatter",
-    )(ga, gm, gsmall)
+    )(*grads)
     return outs[2:]
 
 
@@ -732,12 +750,7 @@
 
     def local_step(*banks):
         grads, weights, firsts, seconds = (banks[n:n + 4] for n in range(0, len(banks), 4))
-        by_wide, by_vec = (x[0].reshape(x.shape[1], DEVICES, -1) for x in grads[2:])
-        by_wide = by_wide.reshape(GROUPS, DEVICES, GROUPS, HALF).transpose(1, 2, 0, 3)
-        by_wide = jnp.pad(by_wide, ((0, 0), (0, 1), (0, TILE - GROUPS), (0, 0))).reshape(DEVICES, SMALL[0], HALF)
-        by_vec = jnp.pad(by_vec.transpose(1, 0, 2), ((0, 0), (0, GROUPS), (0, HALF - by_vec.shape[2])))
-        g_small = jnp.concatenate([by_vec, by_wide], axis=2)
-        gs_a, gs_m, gs_s, clip = reduce_call(grads[0], grads[1], g_small)
+        gs_a, gs_m, gs_s, clip = reduce_call(grads[0], grads[1], grads[3], grads[2])
         attn, mlp, wide, vec = zip(weights, firsts, seconds)
         outs = update_call((gs_a,) + attn, (gs_m,) + mlp, clip, gs_s, *vec, *wide)
         nm_a, nv_a, nm_m, nv_m, nm_vec, nv_vec, nm_wide, nv_wide = outs[:8]

time: 490 us -> 488 us (level)
  no operation moved by 1% of the time
where the time goes in v3:
time: 488 us; the launch traced here: 486 us
  Pallas kernels  474 us (97%)
  local copies, waits for them, and re-layouts  7.22 us (1%)
  starting transfers between devices  4.91 us (1%)
    pallas_call x1, Pallas kernels, reduce_call(): pl.pallas_call(reduce_kernel, out_shape=[jax.ShapeDtypeStruct((A_ROWS, 8...  286 us
    pallas_call x1, Pallas kernels, gather_call(): pl.pallas_call(gather_kernel, out_shape=[jax.ShapeDtypeStruct((PARTS, TIL...  133 us
    pallas_call x3, Pallas kernels, stream_call(): pl.pallas_call(kernel, in_specs=[hbm] * len(ins) + [vmem] * len(vmem_ins)...  37.2 us
    pallas_call x1, Pallas kernels, update_call(): pl.pallas_call(update_kernel, grid=(1,), in_specs=[hbm] * 8 + [whole(x.sh...  17.1 us
  transfers between devices with their start and end apart: 6, of which 0 were waited for; matrix products, arithmetic and copies ran while one was open for 0% of the time, Pallas kernels for 6%

profile of v3, /device:TPU:0, one launch (start us, length us, event | category | flops | bytes accessed | tf_op | source)
XLA Modules:
  0.0 486.5 jit_solution(2577096438896977834)
XLA Ops:
  0.6 285.9 %reduce_scatter.1 = (bf16[12,294912]{1,0:T(8,128)(2,1)}, bf16[6,1179648]{1,0:T(8,128)(2,1)}, f32[12,36864]{1,0:T(8,128)}, f32[6,147456]{1,0:T(8,128)}, f32[32,128]{1,0:T(8,128)}, /*index=5*/f32[8,128]{1,0:T(8,128)}) custom-call(bf16[1,12,589824]{2,1,0:T(8,128)(2,1)} %ga.1, bf16[1,6,2359296]{2,1,0:T(8,128)(2,1)} %gm.1, bf16[1,29,768]{2,1,0:T(8,128)(2,1)} %gvec.1, ...), custom_call_target="tpu_custom_call" | custom-call | tf_op jit(solution)/shard_map/reduce_scatter/pallas_call | solution.py:318
  286.6 17.1 %update.1 = (f32[12,36864]{1,0:T(8,128)}, f32[12,36864]{1,0:T(8,128)}, f32[6,147456]{1,0:T(8,128)}, f32[6,147456]{1,0:T(8,128)}, f32[29,48]{1,0:T(8,128)}, /*ind...) custom-call(f32[12,36864]{1,0:T(8,128)} %get-tuple-element.57.refs_0, ...), custom_call_target="tpu_custom_call" | custom-call | tf_op jit(solution)/shard_map/update/pallas_call | solution.py:441
  303.7 133.3 %all_gather.1 = (bf16[3,8,18432]{2,1,0:T(8,128)(2,1)}, bf16[3,8,18432]{2,1,0:T(8,128)(2,1)}, bf16[3,8,18432]{2,1,0:T(8,128)(2,1)}, bf16[16,3,3,8,18432]{4,3,2,1,...) custom-call(f32[12,36864]{1,0:T(8,128)} %rest_0_.1, ...), custom_call_target="tpu_custom_call" | custom-call | tf_op jit(solution)/shard_map/all_gather/pallas_call | solution.py:616
  437.0 1.3 collective-permute-start
  438.3 1.5 collective-permute-start.1
  439.8 1.5 collective-permute-start.2
  441.3 21.1 %unpack.1 = (bf16[12,589824]{1,0:T(8,128)(2,1)}, bf16[6,2359296]{1,0:T(8,128)(2,1)}, bf16[29,768]{1,0:T(8,128)(2,1)}, bf16[3,3072]{1,0:T(4,128)(2,1)}, f32[29,48]{1,0:T(8,128)}, /*index=5*/f32[3,192]{1,0:T(4,128)}) custom-call(bf16[16,3,3,8,18432]{4,3,2,1,0:T(8,128)(2,1)} %get-tuple-element.74.full, bf16[16,32,128]{2,1,0:T(8,128)(2,1)} %get-tuple-element.75.small_full, ...), custom_call_target="tpu_custom_call" | custom-call | flops 1000000000 | bytes 67108864 | tf_op jit(solution)/shard_map/unpack/pallas_call | solution.py:729
  462.4 0.0 collective-permute-done.refs_0_
  462.4 0.0 collective-permute-done.1.refs_1_
  462.4 0.0 collective-permute-done.2.refs_2_
  462.4 0.0 collective-permute-start.3
  462.5 0.5 collective-permute-start.4
  463.0 0.1 collective-permute-start.5
  463.0 9.6 %unpack_more.1 = (bf16[12,589824]{1,0:T(8,128)(2,1)}, bf16[6,2359296]{1,0:T(8,128)(2,1)}) custom-call(bf16[16,3,3,8,18432]{4,3,2,1,0:T(8,128)(2,1)} %get-tuple-element.74.full, bf16[3,8,18432]{2,1,0:T(8,128)(2,1)} %collective-permute-done.refs_0_, bf16[3,8,18432]{2,1,0:T(8,128)(2,1)} %collective-permute-done.1.refs_1_, ...), custom_call_target="tpu_custom_call", output_to_operand_aliasing={{0}: (4, {}), {1}: (5, {})} | custom-call | flops 1000000000 | bytes 67108864 | tf_op jit(solution)/shard_map/unpack_more/pallas_call | solution.py:729
  472.6 0.0 collective-permute-done.3.refs_3_
  472.6 0.0 collective-permute-done.4.refs_4_
  472.6 0.0 collective-permute-done.5.refs_5_
  472.6 6.6 %unpack_far.1 = (bf16[12,589824]{1,0:T(8,128)(2,1)}, bf16[6,2359296]{1,0:T(8,128)(2,1)}) custom-call(bf16[3,8,18432]{2,1,0:T(8,128)(2,1)} %collective-permute-done.refs_0_, bf16[3,8,18432]{2,1,0:T(8,128)(2,1)} %collective-permute-done.1.refs_1_, bf16[3,8,18432]{2,1,0:T(8,128)(2,1)} %collective-permute-done.2.refs_2_, ...), custom_call_target="tpu_custom_call", output_to_operand_aliasing={{0}: (6, {}), {1}: (7, {})} | custom-call | flops 1000000000 | bytes 67108864 | tf_op jit(solution)/shard_map/unpack_far/pallas_call | solution.py:729
  479.2 3.2 copy.42
  482.5 4.0 copy.43
Async XLA Ops:
  437.0 25.4 %collective-permute-start = (bf16[3,8,18432]{2,1,0:T(8,128)(2,1)}, bf16[3,8,18432]{2,1,0:T(8,128)(2,1)}, u32[]{:S(2)}, u32[]{:S(2)}) collective-permute-start(bf16[3,8,18432]{2,1,0:T(8,128)(2,1)} %get-tuple-element.71), channel_id=1, source_target_pairs={{0,8},{1,9},{2,10},{3,11},{4,12},{5,13},{6,14},{7,15},{8,0},{9,1},... | collective-permute-start | bytes 2654216 | tf_op jit(solution)/shard_map/ppermute | solution.py:743
  438.3 24.1 %collective-permute-start.1 = (bf16[3,8,18432]{2,1,0:T(8,128)(2,1)}, bf16[3,8,18432]{2,1,0:T(8,128)(2,1)}, u32[]{:S(2)}, u32[]{:S(2)}) collective-permute-start(bf16[3,8,18432]{2,1,0:T(8,128)(2,1)} %get-tuple-element.72), channel_id=1, source_target_pairs={{0,2},{1,3},{2,0},{3,1},{4,6},{5,7},{6,4},{7,5},{8,10},{9,11},{10,... | collective-permute-start | bytes 2654216 | tf_op jit(solution)/shard_map/ppermute | solution.py:743
  439.8 22.6 %collective-permute-start.2 = (bf16[3,8,18432]{2,1,0:T(8,128)(2,1)}, bf16[3,8,18432]{2,1,0:T(8,128)(2,1)}, u32[]{:S(2)}, u32[]{:S(2)}) collective-permute-start(bf16[3,8,18432]{2,1,0:T(8,128)(2,1)} %get-tuple-element.73), channel_id=1, source_target_pairs={{0,4},{1,5},{2,6},{3,7},{4,0},{5,1},{6,2},{7,3},{8,12},{9,13},{10,... | collective-permute-start | bytes 2654216 | tf_op jit(solution)/shard_map/ppermute | solution.py:743
  462.4 10.2 %collective-permute-start.3 = (bf16[3,8,18432]{2,1,0:T(8,128)(2,1)}, bf16[3,8,18432]{2,1,0:T(8,128)(2,1)}, u32[]{:S(2)}, u32[]{:S(2)}) collective-permute-start(bf16[3,8,18432]{2,1,0:T(8,128)(2,1)} %collective-permute-done.refs_0_), channel_id=1, source_target_pairs={{0,1},{1,0},{2,3},{3,2},{4,5},{5,4},{6,7},{7,6},{8,9},{9,8},{10,11... | collective-permute-start | bytes 2654216 | tf_op jit(solution)/shard_map/ppermute | solution.py:743
  462.5 10.2 %collective-permute-start.4 = (bf16[3,8,18432]{2,1,0:T(8,128)(2,1)}, bf16[3,8,18432]{2,1,0:T(8,128)(2,1)}, u32[]{:S(2)}, u32[]{:S(2)}) collective-permute-start(bf16[3,8,18432]{2,1,0:T(8,128)(2,1)} %collective-permute-done.1.refs_1_), channel_id=1, source_target_pairs={{0,1},{1,0},{2,3},{3,2},{4,5},{5,4},{6,7},{7,6},{8,9},{9,8},{10,11... | collective-permute-start | bytes 2654216 | tf_op jit(solution)/shard_map/ppermute | solution.py:743
  463.0 9.7 %collective-permute-start.5 = (bf16[3,8,18432]{2,1,0:T(8,128)(2,1)}, bf16[3,8,18432]{2,1,0:T(8,128)(2,1)}, u32[]{:S(2)}, u32[]{:S(2)}) collective-permute-start(bf16[3,8,18432]{2,1,0:T(8,128)(2,1)} %collective-permute-done.2.refs_2_), channel_id=1, source_target_pairs={{0,1},{1,0},{2,3},{3,2},{4,5},{5,4},{6,7},{7,6},{8,9},{9,8},{10,11... | collective-permute-start | bytes 2654216 | tf_op jit(solution)/shard_map/ppermute | solution.py:743
